TPU v7x, 1024 devices: a whole 4x8x16 slice. The times are simulated.
1024 devices in a mesh: fsdp: 16 (over z_lo, core), roll: 64 (over y, z_hi, x).
Axes of the slice: x: 4, y: 8, z: 16 (z_hi: 2, z_lo: 8; z = z_hi * 8 + z_lo), core: 2. Of those that a mesh axis runs over, the one named last changes fastest.
Arguments:
- trainer_weights: bfloat16 [64, 1024, 8192], P('roll', None, 'fsdp'), may hold values from -0.09375 to 0.09375
- power_table: int32 [8192, 512], P('fsdp'), may hold values from 1 to 250, as said below
- assign: int32 [2], replicated, may hold values from 0 to 63
Outputs:
- rollout_weights: bfloat16 [64, 2, 1024, 8192], P('roll', None, 'fsdp')
- fingerprint: bfloat16 [64, 2, 1024, 512], P('roll', None, 'fsdp')
Inputs may be any that keep to these rules, and one draw needn't show every extreme that they name: `power_table`: each entry is, modulo 251, a row factor times a column factor times the column's generator raised to the row index.
All inputs are finite; a program needn't handle non-finite values.
Results may differ from a plain program's by a relative error of at most 0.019.
Values may be sent and summed in bfloat16 or wider, within the bound.
No kernel may reach another device: no remote copies, remote signals or barrier semaphores. Data moves between devices by JAX's collectives and lax.ppermute only.
A program may use at most 32 MiB of HBM per device.

v0:
```python
import jax.numpy as jnp
from jax import lax

N_FSDP = 16
N_ROLL = 64
D = 8192
COLS = 1024
FP = 512
LAYERS = 2


spread_inverse = 1.0 / 72.0


def reference(trainer_weights, power_table, assign):
    centered = (power_table - 125).astype(jnp.float32)
    blocks = centered.reshape(N_FSDP, D // N_FSDP, FP)
    rollout = []
    prints = []
    for number in range(LAYERS):
        chosen = lax.dynamic_index_in_dim(trainer_weights, assign[number], 0, keepdims=False)
        rollout.append(chosen)
        pieces = chosen.astype(jnp.float32).reshape(COLS, N_FSDP, D // N_FSDP)
        partial_value = jnp.einsum(
            "cjd,jdf->jcf", pieces, blocks, precision=lax.Precision.HIGHEST
        ).astype(jnp.bfloat16)
        summed = jnp.sum(partial_value.astype(jnp.float32), axis=0)
        prints.append((summed * spread_inverse).astype(jnp.bfloat16))
    stacked = jnp.stack(rollout)
    printed = jnp.stack(prints)
    copies = jnp.broadcast_to(stacked[None], (N_ROLL,) + stacked.shape)
    print_copies = jnp.broadcast_to(printed[None], (N_ROLL,) + printed.shape)
    return (copies, print_copies)


def solution(mesh):
    return reference
```

profile of v0, /device:TPU:6, one launch (start us, length us, event | category | flops | bytes accessed | tf_op | source)
XLA Modules:
  0.0 667.5 jit_solution(17020964548793387991)
XLA Ops:
  7.2 0.0 copy-start.2
  7.2 0.0 copy-start
  7.2 27.6 %all-to-all-start = ((bf16[1,64,16,512]{3,2,0,1:T(8,128)(2,1)}), bf16[1,64,16,512]{3,2,0,1:T(8,128)(2,1)S(1)}, u32[]{:S(2)}, u32[]{:S(2)}) async-start(bf16[1,64,16,512]{3,2,0,1:T(8,128)(2,1)} %bitcast.29), calls=%async_computation | async-start | bytes 2097152 | tf_op jit(solution)/call_exported
  34.8 0.0 all-gather.9.cloned.1.call-start
  34.9 0.0 copy-done.2
  34.9 0.6 fusion.14
  39.3 24.4 %all-to-all-done = bf16[1,64,16,512]{3,2,0,1:T(8,128)(2,1)S(1)} async-done(((bf16[1,64,16,512]{3,2,0,1:T(8,128)(2,1)}), bf16[1,64,16,512]{3,2,0,1:T(8,128)(2,1)S(1)}, u32[]{:S(2)}, u32[]{:S(2)}) %all-to-all-start) | async-done | bytes 1048608 | tf_op jit(solution)/call_exported
  63.7 0.6 constant_dynamic-slice_fusion.1
  64.3 0.0 all-gather.9.cloned.1.call-update
  64.3 0.0 all-gather.7.cloned.1.call-start
  64.4 0.7 all-gather.7.cloned.1.call-update
  65.1 0.0 reduce-scatter.9.cloned.1.call-start
  65.1 186.9 %all-gather.9.cloned.1.call-done = bf16[1,1,1024,512]{3,2,1,0:T(8,128)(2,1)} async-done(((bf16[1,1,16,512]{3,2,1,0:T(8,128)(2,1)}), bf16[1,1,1024,512]{3,2,1,0:T(8,128)(2,1)}) %all-gather.9.cloned.1.call-update) | async-done | bytes 1048592 | tf_op jit(solution)/jit(dynamic_index_in_dim)/dynamic_slice | solution.py:21
  252.0 0.0 copy-done
  252.0 4.5 fusion
  256.5 0.0 reduce-scatter.9.cloned.1.call-update
  256.5 152.6 %all-gather.7.cloned.1.call-done = bf16[1,1,1024,512]{3,2,1,0:T(8,128)(2,1)} async-done(((bf16[1,1,16,512]{3,2,1,0:T(8,128)(2,1)}), bf16[1,1,1024,512]{3,2,1,0:T(8,128)(2,1)}) %all-gather.7.cloned.1.call-update) | async-done | bytes 1048592 | tf_op jit(solution)/jit(dynamic_index_in_dim)/dynamic_slice | solution.py:21
  409.1 0.0 copy-done.1
  409.1 1.4 pad_maximum_fusion
  410.5 1.5 copy.3
  412.1 3.7 all-to-all-start.1
  415.8 0.0 reduce-scatter.7.cloned.1.call-start
  415.8 4.4 fusion.1
  420.3 0.0 reduce-scatter.7.cloned.1.call-update
  420.3 117.7 %reduce-scatter.9.cloned.1.call-done = f32[64,512]{1,0:T(8,128)} async-done(((f32[1024,512]{1,0:T(8,128)}), f32[64,512]{1,0:T(8,128)}) %reduce-scatter.9.cloned.1.call-update) | async-done | bytes 131088
  538.0 0.9 fusion.11
  538.9 113.7 %reduce-scatter.7.cloned.1.call-done = f32[64,512]{1,0:T(8,128)} async-done(((f32[1024,512]{1,0:T(8,128)}), f32[64,512]{1,0:T(8,128)}) %reduce-scatter.7.cloned.1.call-update) | async-done | bytes 131088
  652.7 0.9 fusion.10
  653.6 0.7 maximum_bitcast_fusion
  654.3 0.0 all-to-all-done.1
  654.3 2.5 copy.4
  656.8 4.2 reshape.72
  (1 shorter events, 0.0 us)
Async XLA Ops:
  7.2 27.7 %copy-start.2 = (s32[2]{0:T(128)S(1)}, s32[2]{0:T(128)}, u32[]{:S(2)}) copy-start(s32[2]{0:T(128)} %param.1) | copy-start | bytes 28
  7.2 244.9 %copy-start = (s32[512,512]{1,0:T(8,128)S(1)}, s32[512,512]{1,0:T(8,128)}, u32[]{:S(2)}) copy-start(s32[512,512]{1,0:T(8,128)} %param.2) | copy-start | bytes 3145732
  7.2 56.5 %all-to-all-start = ((bf16[1,64,16,512]{3,2,0,1:T(8,128)(2,1)}), bf16[1,64,16,512]{3,2,0,1:T(8,128)(2,1)S(1)}, u32[]{:S(2)}, u32[]{:S(2)}) async-start(bf16[1,64,16,512]{3,2,0,1:T(8,128)(2,1)} %bitcast.29), calls=%async_computation | async-start | bytes 2097152 | tf_op jit(solution)/call_exported
  34.8 217.2 %all-gather.9.cloned.1.call-start = ((), (), s32[]{:S(2)}) async-start(), calls=%async_computation.5 | async-start | bytes 1064960 | tf_op jit(solution)/jit(dynamic_index_in_dim)/dynamic_slice | solution.py:21
  64.3 344.8 %all-gather.7.cloned.1.call-start = ((), (), s32[]{:S(2)}) async-start(), calls=%async_computation.4 | async-start | bytes 1064960 | tf_op jit(solution)/jit(dynamic_index_in_dim)/dynamic_slice | solution.py:21
  65.1 472.9 %reduce-scatter.9.cloned.1.call-start = ((), (), s32[]{:S(2)}) async-start(), calls=%async_computation.7 | async-start | bytes 2228224
  256.5 152.6 %copy-start.1 = (bf16[1,1,1024,512]{3,2,1,0:T(8,128)(2,1)S(1)}, bf16[1,1,1024,512]{3,2,1,0:T(8,128)(2,1)}, u32[]{:S(2)}) copy-start(bf16[1,1,1024,512]{3,2,1,0:T(8,128)(2,1)} %all-gather.9.cloned.1.call-done) | copy-start | bytes 3145732
  412.1 242.2 %all-to-all-start.1 = ((bf16[2,16,64,512]{3,2,0,1:T(8,128)(2,1)}), bf16[2,16,64,512]{3,2,0,1:T(8,128)(2,1)S(1)}, u32[]{:S(2)}, u32[]{:S(2)}) async-start(bf16[2,16,64,512]{3,2,0,1:T(8,128)(2,1)} %copy.3), calls=%async_computation.1 | async-start | bytes 4194304 | tf_op jit(solution)/stack | solution.py:29
  415.8 236.9 %reduce-scatter.7.cloned.1.call-start = ((), (), s32[]{:S(2)}) async-start(), calls=%async_computation.6 | async-start | bytes 2228224
Sparse Core Ops, SparseCore 0:
  64.5 187.5 all-gather.8
  258.4 150.6 all-gather.6
  412.5 125.4 reduce-scatter.8
  541.3 111.3 reduce-scatter.6
where the time goes:
time: 668 us; the launch traced here: 667 us
  waiting for transfers between devices  596 us (89%)
  starting transfers between devices  31.5 us (5%)
  between operations  17.7 us (3%)
  local copies, waits for them, and re-layouts  9.44 us (1%)
  matrix products  8.88 us (1%)
    dynamic_slice x2, waiting for transfers between devices, reference(): lax.dynamic_index_in_dim(trainer_weights, assign[number], 0, keepdims=False)  339 us
    unnamed x6, waiting for transfers between devices  232 us
    another operation x1, starting transfers between devices  27.6 us
    another operation x1, waiting for transfers between devices  24.4 us
  transfers between devices with their start and end apart: 6, of which 5 were waited for; matrix products, arithmetic and copies ran while one was open for 2% of the time, Pallas kernels for 0%

commit v1 on v0

v1 whole, which is shorter than its diff:
```python
import jax
import jax.numpy as jnp
from jax import lax
from jax.sharding import Mesh, PartitionSpec as P

LAYERS = 2
spread_inverse = 1.0 / 72.0


def solution(mesh):
    n_y, n_zh, n_x = 8, 2, 4
    n_zl, n_co = 8, 2
    fine = Mesh(
        mesh.devices.reshape(n_zl, n_co, n_y, n_zh, n_x), ("zl", "co", "y", "zh", "x")
    )
    n_f = n_zl * n_co
    n_k = n_y * n_x

    def body(w, table, assign):
        cols = w.shape[2]
        rows = w.shape[1] // n_f
        c = rows // n_k
        pieces = w.reshape(n_f, n_k, c, cols).transpose(1, 0, 2, 3)
        got = lax.all_to_all(pieces, ("y", "x"), 0, 0, tiled=True)
        centered = (table - 125).astype(jnp.bfloat16)
        owner_y = assign // (n_zh * n_x)
        owner_zh = assign // n_x % n_zh
        owner_x = assign % n_x
        owner_k = owner_y * n_x + owner_x
        chosen = jnp.stack(
            [lax.dynamic_index_in_dim(got, owner_k[l], 0, keepdims=False) for l in range(LAYERS)]
        )
        part = lax.dot_general(
            chosen.reshape(LAYERS * n_f * c, cols), centered, (((1,), (0,)), ((), ())),
            preferred_element_type=jnp.float32,
        ).astype(jnp.bfloat16).reshape(LAYERS, n_f, c, -1)
        both = jnp.stack([chosen, part], axis=0)
        both = both.transpose(2, 0, 1, 3, 4)
        send = jnp.concatenate([both] * n_zh, axis=0)
        recv = lax.all_to_all(send, ("zh", "zl", "co"), 0, 0, tiled=True)
        recv = recv.reshape(n_zh, n_f, 2, LAYERS, c, cols)
        half = jnp.stack(
            [lax.dynamic_index_in_dim(recv[:, :, :, l], owner_zh[l], 0, keepdims=False) for l in range(LAYERS)],
            axis=2,
        )
        mine = half[:, 0].transpose(1, 2, 0, 3).reshape(LAYERS, c, n_f * cols)
        summed = jnp.sum(half[:, 1].astype(jnp.float32), axis=0)
        prints = (summed * spread_inverse).astype(jnp.bfloat16)
        line = jnp.concatenate([mine, prints], axis=2)
        by_y = lax.all_to_all(jnp.stack([line] * n_y), "y", 0, 0, tiled=True)
        full = lax.all_to_all(jnp.stack([by_y] * n_x), "x", 0, 0, tiled=True)
        full = full.transpose(2, 1, 0, 3, 4).reshape(1, LAYERS, rows, n_f * cols + cols)
        return full[..., : n_f * cols], full[..., n_f * cols :]

    roll = ("y", "zh", "x")
    fsdp = ("zl", "co")
    return jax.shard_map(
        body, mesh=fine, in_specs=(P(roll, None, fsdp), P(fsdp, None), P(None)),
        out_specs=(P(roll, None, fsdp, None), P(roll, None, fsdp, None)), check_vma=False,
    )
```

time: 668 us -> 148 us (0.22)
  waiting for transfers between devices: 596 us -> 36 us
  blocking collectives: 0 us -> 50.4 us
  between operations: 17.7 us -> 8.39 us
  matrix products: 8.88 us -> 0.24 us
    dynamic_slice x2 -> x0, waiting for transfers between devices: 339 us -> none  [reference(): lax.dynamic_index_in_dim(trainer_weights, assign[number], 0, keepdims=False)]
    unnamed x6 -> x0, waiting for transfers between devices: 232 us -> none
    all_to_all x0 -> x2, blocking collectives: none -> 50.4 us  [the longest x1 29.5 us: body(): full = lax.all_to_all(jnp.stack([by_y] * n_x), 'x', 0, 0, tiled=True)]
    all_to_all x0 -> x2, waiting for transfers between devices: none -> 36 us  [the longest x1 19.1 us: body(): recv = lax.all_to_all(send, ('zh', 'zl', 'co'), 0, 0, tiled=True)]
    all_to_all x0 -> x2, starting transfers between devices: none -> 35.8 us  [the longest x1 19.1 us: body(): recv = lax.all_to_all(send, ('zh', 'zl', 'co'), 0, 0, tiled=True)]
    another operation x2 -> x0, starting transfers between devices: 31.3 us -> none
    another operation x2 -> x0, waiting for transfers between devices: 24.4 us -> none
    dot_general x2 -> x1, matrix products: 8.88 us -> 0.24 us  [body(): lax.dot_general(chosen.reshape(LAYERS * n_f * c, cols), centered, (((1,),...]
  transfers between devices with their start and end apart: 6 -> 2, of which waited for: 5 -> 2; matrix products, arithmetic and copies ran while one was open for 2% -> 0% of each run, Pallas kernels for 0% -> 0%
where the time goes in v1:
time: 148 us; the launch traced here: 147 us
  blocking collectives  50.4 us (34%)
  waiting for transfers between devices  36 us (24%)
  starting transfers between devices  35.8 us (24%)
  local copies, waits for them, and re-layouts  15.2 us (10%)
  between operations  8.39 us (6%)
    all_to_all x1, blocking collectives, body(): full = lax.all_to_all(jnp.stack([by_y] * n_x), 'x', 0, 0, tiled=True)  29.5 us
    all_to_all x1, blocking collectives, body(): by_y = lax.all_to_all(jnp.stack([line] * n_y), 'y', 0, 0, tiled=True)  20.9 us
    all_to_all x1, starting transfers between devices, body(): recv = lax.all_to_all(send, ('zh', 'zl', 'co'), 0, 0, tiled=True)  19.1 us
    all_to_all x1, waiting for transfers between devices, body(): recv = lax.all_to_all(send, ('zh', 'zl', 'co'), 0, 0, tiled=True)  19.1 us
    all_to_all x1, waiting for transfers between devices, body(): got = lax.all_to_all(pieces, ('y', 'x'), 0, 0, tiled=True)  16.9 us
    all_to_all x1, starting transfers between devices, body(): got = lax.all_to_all(pieces, ('y', 'x'), 0, 0, tiled=True)  16.7 us
    unnamed x8, local copies, waits for them, and re-layouts  3.2 us
  transfers between devices with their start and end apart: 2, of which 2 were waited for; matrix products, arithmetic and copies ran while one was open for 0% of the time, Pallas kernels for 0%

profile of v1, /device:TPU:6, one launch (start us, length us, event | category | flops | bytes accessed | tf_op | source)
XLA Modules:
  0.0 146.8 jit_solution(343376675657446186)
XLA Ops:
  0.6 1.5 %reshape.30 = bf16[16,32,2,512]{3,2,1,0:T(2,128)(2,1)S(1)} reshape(bf16[1,1024,512]{2,1,0:T(8,128)(2,1)} %param.3) | data formatting | bytes 2097152 | tf_op jit(solution)/shard_map/reshape | solution.py:23
  2.1 0.0 copy-start.1
  2.1 0.0 copy-start
  2.1 2.1 %copy.23 = bf16[32,16,2,512]{3,2,1,0:T(2,128)(2,1)} copy(bf16[32,16,2,512]{3,2,0,1:T(2,128)(2,1)S(1)} %bitcast.28) | data formatting | bytes 2097152 | tf_op jit(solution)/shard_map/transpose | solution.py:23
  4.2 16.7 %all-to-all-start = ((bf16[32,16,2,512]{3,2,1,0:T(2,128)(2,1)}), bf16[32,16,2,512]{3,2,1,0:T(2,128)(2,1)S(1)}, u32[]{:S(2)}, u32[]{:S(2)}) async-start(bf16[32,16,2,512]{3,2,1,0:T(2,128)(2,1)} %copy.23), calls=%async_computation | async-start | bytes 2097152 | tf_op jit(solution)/shard_map/all_to_all | solution.py:24
  20.9 0.0 copy-done.1
  21.0 0.7 fusion.7
  25.5 16.9 %all-to-all-done = bf16[32,16,2,512]{3,2,1,0:T(2,128)(2,1)S(1)} async-done(((bf16[32,16,2,512]{3,2,1,0:T(2,128)(2,1)}), bf16[32,16,2,512]{3,2,1,0:T(2,128)(2,1)S(1)}, u32[]{:S(2)}, u32[]{:S(2)}) %all-to-all-start) | async-done | bytes 1048608 | tf_op jit(solution)/shard_map/all_to_all | solution.py:24
  42.5 0.1 fusion.10
  42.6 0.1 pad_maximum_fusion.3
  42.8 0.0 copy-done
  42.8 0.2 convolution_convert_fusion
  43.1 0.2 maximum_bitcast_fusion
  43.3 0.2 pad_maximum_fusion
  43.5 0.9 copy.24
  44.3 19.1 %all-to-all-start.1 = ((bf16[32,2,2,2,512]{4,3,2,1,0:T(2,128)(2,1)}), bf16[32,2,2,2,512]{4,3,2,1,0:T(2,128)(2,1)S(1)}, u32[]{:S(2)}, u32[]{:S(2)}) async-start(bf16[32,2,2,2,512]{4,3,2,1,0:T(2,128)(2,1)} %copy.24), calls=%async_computation.1 | async-start | bytes 524288 | tf_op jit(solution)/shard_map/all_to_all | solution.py:40
  67.1 19.1 %all-to-all-done.1 = bf16[32,2,2,2,512]{4,3,2,1,0:T(2,128)(2,1)S(1)} async-done(((bf16[32,2,2,2,512]{4,3,2,1,0:T(2,128)(2,1)}), bf16[32,2,2,2,512]{4,3,2,1,0:T(2,128)(2,1)S(1)}, u32[]{:S(2)}, u32[]{:S(2)}) %all-to-all-start.1) | async-done | bytes 262176 | tf_op jit(solution)/shard_map/all_to_all | solution.py:40
  86.2 0.2 fusion.6
  86.4 0.1 constant_dynamic-slice_fusion.1
  86.4 0.1 constant_dynamic-slice_fusion
  86.6 0.1 pad_maximum_fusion.1
  86.7 0.3 stack.44
  87.0 20.9 %all_to_all.20 = bf16[8,2,2,8704]{3,2,1,0:T(2,128)(2,1)S(1)} all-to-all(bf16[8,2,2,8704]{3,2,1,0:T(2,128)(2,1)S(1)} %stack.44), channel_id=1, replica_groups=mesh['zl'=8,'co'=2,'y'=8,'zh'=2,'x'=4] {'y'}, dimensions={0} | all-to-all | bytes 1114112 | tf_op jit(solution)/shard_map/all_to_all | solution.py:50
  107.9 0.4 copy.27
  108.3 1.1 stack.45
  109.4 29.5 %all_to_all.21 = bf16[4,8,2,2,8704]{4,3,1,2,0:T(2,128)(2,1)S(1)} all-to-all(bf16[4,8,2,2,8704]{4,3,1,2,0:T(2,128)(2,1)S(1)} %stack.45), channel_id=1, replica_groups=mesh['zl'=8,'co'=2,'y'=8,'zh'=2,'x'=4] {'x'}, dimensions={0} | all-to-all | bytes 4456448 | tf_op jit(solution)/shard_map/all_to_all | solution.py:51
  138.9 2.3 %copy.28 = bf16[2,8,4,2,8704]{4,0,3,2,1:T(2,128)(2,1)S(1)} copy(bf16[2,8,4,2,8704]{4,3,1,0,2:T(2,128)(2,1)S(1)} %bitcast.27) | data formatting | bytes 4456448 | tf_op jit(solution)/shard_map/transpose | solution.py:52
  141.2 0.1 slice.45
  141.3 2.3 %slice.44 = bf16[1,2,64,8192]{3,1,2,0:T(2,128)(2,1)S(1)} slice(bf16[1,2,64,8704]{3,1,2,0:T(2,128)(2,1)S(1)} %bitcast.26), slice={[0:1], [0:2], [0:64], [0:8192]} | slice | bytes 4194304 | tf_op jit(solution)/shard_map/slice | solution.py:53
  143.6 2.5 %copy.29 = bf16[1,2,64,8192]{3,2,1,0:T(8,128)(2,1)} copy(bf16[1,2,64,8192]{3,1,2,0:T(2,128)(2,1)S(1)} %slice.44) | data formatting | bytes 4194304
  146.1 0.7 copy.30
  (10 shorter events, 0.2 us)
Async XLA Ops:
  2.1 18.8 %copy-start.1 = (s32[2]{0:T(128)S(1)}, s32[2]{0:T(128)}, u32[]{:S(2)}) copy-start(s32[2]{0:T(128)} %param.5) | copy-start | bytes 28
  2.1 40.7 %copy-start = (s32[512,512]{1,0:T(8,128)S(1)}, s32[512,512]{1,0:T(8,128)}, u32[]{:S(2)}) copy-start(s32[512,512]{1,0:T(8,128)} %param.4) | copy-start | bytes 3145732
  4.2 38.3 %all-to-all-start = ((bf16[32,16,2,512]{3,2,1,0:T(2,128)(2,1)}), bf16[32,16,2,512]{3,2,1,0:T(2,128)(2,1)S(1)}, u32[]{:S(2)}, u32[]{:S(2)}) async-start(bf16[32,16,2,512]{3,2,1,0:T(2,128)(2,1)} %copy.23), calls=%async_computation | async-start | bytes 2097152 | tf_op jit(solution)/shard_map/all_to_all | solution.py:24
  44.3 41.8 %all-to-all-start.1 = ((bf16[32,2,2,2,512]{4,3,2,1,0:T(2,128)(2,1)}), bf16[32,2,2,2,512]{4,3,2,1,0:T(2,128)(2,1)S(1)}, u32[]{:S(2)}, u32[]{:S(2)}) async-start(bf16[32,2,2,2,512]{4,3,2,1,0:T(2,128)(2,1)} %copy.24), calls=%async_computation.1 | async-start | bytes 524288 | tf_op jit(solution)/shard_map/all_to_all | solution.py:40

commit v2 on v0

v2 whole, which is shorter than its diff:
```python
import jax
import jax.numpy as jnp
import numpy as np
from jax import lax
from jax.experimental import pallas as pl
from jax.experimental.pallas import tpu as pltpu
from jax.sharding import Mesh, PartitionSpec as P

D = 8192
COLS = 1024
FP = 512
LAYERS = 2
N_Y, N_ZH, N_X = 8, 2, 4
N_ZL, N_CO = 8, 2
N_F = N_ZL * N_CO
N_K = N_Y * N_X
WIDE = D // N_F
ROWS = COLS // N_F
C = ROWS // N_K
TALL = N_Y * C
LINE = D // 2 + FP // 2

spread_inverse = 1.0 / 72.0


def selection(source, count):
    return (np.asarray(source)[:, None] == np.arange(count)[None, :]).astype(jnp.bfloat16)


def regroup(order_ref, w_ref, out_ref):
    flat = w_ref[...].reshape(N_F * TALL, WIDE)
    moved = jnp.dot(order_ref[...], flat, preferred_element_type=jnp.float32)
    out_ref[...] = moved.astype(jnp.bfloat16).reshape(out_ref.shape)


def pick(owner_ref, order_ref, got_ref, centered_ref, out_ref):
    chosen = jnp.concatenate([got_ref[owner_ref[0]], got_ref[owner_ref[1]]], axis=0)
    part = jnp.dot(chosen, centered_ref[...], preferred_element_type=jnp.float32)
    both = jnp.concatenate([chosen, part.astype(jnp.bfloat16)], axis=0)
    moved = jnp.dot(order_ref[...], both, preferred_element_type=jnp.float32).astype(jnp.bfloat16)
    for half in range(N_ZH):
        out_ref[half] = moved


def settle(half_ref, recv_ref, out_ref):
    recv = recv_ref[...]
    row = lax.broadcasted_iota(jnp.int32, (64, 256), 0)
    col = lax.broadcasted_iota(jnp.int32, (64, 256), 1)
    layer = row // 2 % 2
    z_hi = jnp.where(layer == 0, half_ref[0], half_ref[1])
    source = z_hi * 128 + (row // 4 % 2 * 8 + row // 8) * 8 + row % 4
    weights = jnp.dot(
        jnp.where(col == source, 1.0, 0.0).astype(jnp.bfloat16), recv,
        preferred_element_type=jnp.float32,
    )
    row8, col8 = row[:8], col[:8]
    hit = (col8 // 128 == z_hi[:8]) & (col8 % 8 == 4 + row8 % 4)
    summed = jnp.dot(
        jnp.where(hit, 1.0, 0.0).astype(jnp.bfloat16), recv, preferred_element_type=jnp.float32
    ) * spread_inverse
    upper = lax.broadcasted_iota(jnp.int32, (8, FP // 2), 0) < 4
    prints = jnp.where(upper, summed[:, : FP // 2], summed[:, FP // 2 :]).astype(jnp.bfloat16)
    for y in range(N_Y):
        for low in range(N_F // 2):
            out_ref[y, :, WIDE * low : WIDE * (low + 1)] = weights[8 * low : 8 * low + 8].astype(jnp.bfloat16)
        out_ref[y, :, D // 2 :] = prints


def lift(order_ref, line_ref, out_ref):
    for j in range(LINE // 256):
        moved = jnp.dot(
            order_ref[...], line_ref[:, 256 * j : 256 * j + 256], preferred_element_type=jnp.float32
        ).astype(jnp.bfloat16)
        for h in range(2):
            at = h * (D // 2) + 256 * j if j < D // 512 else D + 256 * h
            for l in range(LAYERS):
                r = (h * LAYERS + l) * TALL
                for x in range(N_X):
                    out_ref[x, l, :, at : at + 256] = moved[r : r + TALL]


def finish(full_ref, w_ref, f_ref):
    w_ref[0] = full_ref[0, 0, :, :D]
    f_ref[0] = full_ref[0, 0, :, D:]


def whole(shape):
    return pl.BlockSpec(shape, lambda *_: (0,) * len(shape))


def shape_of(*dims):
    return jax.ShapeDtypeStruct(dims, jnp.bfloat16)


VMEM = pl.BlockSpec(memory_space=pltpu.VMEM)
SMEM = pl.BlockSpec(memory_space=pltpu.SMEM)


def regrouped(w):
    spot = np.arange(N_F * TALL)
    order = selection(spot // C % N_F * TALL + spot // (N_F * C) * C + spot % C, N_F * TALL)
    return pl.pallas_call(
        regroup,
        grid=(N_X,),
        in_specs=[whole(order.shape), pl.BlockSpec((N_F, 1, TALL, WIDE), lambda x: (0, x, 0, 0))],
        out_specs=pl.BlockSpec((N_Y, 1, N_F * C, WIDE), lambda x: (0, x, 0, 0)),
        out_shape=shape_of(N_Y, N_X, N_F * C, WIDE),
        name="regroup",
    )(order, w.reshape(N_F, N_X, TALL, WIDE))


def picked(owner_k, got, centered):
    spot = np.arange(128)
    order = selection(spot // 4 % 2 * 64 + spot // 2 % 2 * 32 + spot // 8 * 2 + spot % 2, 128)
    return pl.pallas_call(
        pick,
        in_specs=[SMEM, VMEM, VMEM, VMEM],
        out_specs=VMEM,
        out_shape=shape_of(N_ZH, 128, WIDE),
        name="pick",
    )(owner_k, order, got, centered)


def settled(owner_zh, recv):
    return pl.pallas_call(
        settle,
        in_specs=[SMEM, VMEM],
        out_specs=VMEM,
        out_shape=shape_of(N_Y, 8, LINE),
        name="settle",
    )(owner_zh, recv)


def lifted(line):
    spot = np.arange(64)
    order = selection(spot // 2 % 8 * 8 + spot // 32 * 4 + spot // 16 % 2 * 2 + spot % 2, 64)
    return pl.pallas_call(
        lift,
        in_specs=[VMEM, VMEM],
        out_specs=VMEM,
        out_shape=shape_of(N_X, LAYERS, TALL, D + FP),
        name="lift",
    )(order, line)


def finished(full):
    return pl.pallas_call(
        finish,
        grid=(LAYERS, N_X),
        in_specs=[pl.BlockSpec((1, 1, TALL, D + FP), lambda l, x: (x, l, 0, 0))],
        out_specs=[
            pl.BlockSpec((1, TALL, D), lambda l, x: (l, x, 0)),
            pl.BlockSpec((1, TALL, FP), lambda l, x: (l, x, 0)),
        ],
        out_shape=[shape_of(LAYERS, ROWS, D), shape_of(LAYERS, ROWS, FP)],
        name="finish",
    )(full)


def solution(mesh):
    fine = Mesh(
        mesh.devices.reshape(N_ZL, N_CO, N_Y, N_ZH, N_X), ("zl", "co", "y", "zh", "x")
    )

    def body(w, table, assign):
        got = lax.all_to_all(
            regrouped(w).reshape(N_K, N_F * C, WIDE), ("y", "x"), 0, 0, tiled=True
        )
        centered = (table - 125).astype(jnp.bfloat16)
        owner_zh = assign // N_X % N_ZH
        owner_k = assign // (N_ZH * N_X) * N_X + assign % N_X
        send = picked(owner_k, got, centered)
        recv = lax.all_to_all(
            send.reshape(N_ZH * N_F, 8, WIDE), ("zh", "zl", "co"), 0, 0, tiled=True
        )
        lines = settled(owner_zh, recv.reshape(N_ZH * 128, WIDE))
        by_y = lax.all_to_all(lines, "y", 0, 0, tiled=True)
        full = lax.all_to_all(lifted(by_y.reshape(64, LINE)), "x", 0, 0, tiled=True)
        w_out, f_out = finished(full)
        return w_out[None], f_out[None]

    roll = ("y", "zh", "x")
    fsdp = ("zl", "co")
    return jax.shard_map(
        body, mesh=fine, in_specs=(P(roll, None, fsdp), P(fsdp, None), P(None)),
        out_specs=(P(roll, None, fsdp, None), P(roll, None, fsdp, None)), check_vma=False,
    )
```

time: 668 us -> 153 us (0.23)
  waiting for transfers between devices: 596 us -> 20 us
  blocking collectives: 0 us -> 94.6 us
  between operations: 17.7 us -> 0.67 us
  Pallas kernels: 0 us -> 16.8 us
  starting transfers between devices: 31.5 us -> 16.7 us
  matrix products: 8.88 us -> 0 us
  local copies, waits for them, and re-layouts: 9.44 us -> 0.98 us
    dynamic_slice x2 -> x0, waiting for transfers between devices: 339 us -> none  [reference(): lax.dynamic_index_in_dim(trainer_weights, assign[number], 0, keepdims=False)]
    unnamed x6 -> x0, waiting for transfers between devices: 232 us -> none
    all_to_all x0 -> x3, blocking collectives: none -> 94.6 us  [the longest x1 41.9 us: body(): lax.all_to_all(send.reshape(N_ZH * N_F, 8, WIDE), ('zh', 'zl', 'co'), 0,...]
    another operation x2 -> x0, starting transfers between devices: 31.3 us -> none
    another operation x2 -> x0, waiting for transfers between devices: 24.4 us -> none
    all_to_all x0 -> x1, waiting for transfers between devices: none -> 20 us  [body(): lax.all_to_all(regrouped(w).reshape(N_K, N_F * C, WIDE), ('y', 'x'), 0, 0...]
    pallas_call x0 -> x5, Pallas kernels: none -> 16.8 us  [the longest x1 5.69 us: finished(): pl.pallas_call(finish, grid=(LAYERS, N_X), in_specs=[pl.BlockSpec((1, 1,...]
    all_to_all x0 -> x1, starting transfers between devices: none -> 16.7 us  [body(): lax.all_to_all(regrouped(w).reshape(N_K, N_F * C, WIDE), ('y', 'x'), 0, 0...]
  transfers between devices with their start and end apart: 6 -> 1, of which waited for: 5 -> 1; matrix products, arithmetic and copies ran while one was open for 2% -> 1% of each run, Pallas kernels for 0% -> 0%
where the time goes in v2:
time: 153 us; the launch traced here: 151 us
  blocking collectives  94.6 us (62%)
  waiting for transfers between devices  20 us (13%)
  Pallas kernels  16.8 us (11%)
  starting transfers between devices  16.7 us (11%)
    all_to_all x1, blocking collectives, body(): lax.all_to_all(send.reshape(N_ZH * N_F, 8, WIDE), ('zh', 'zl', 'co'), 0,...  41.9 us
    all_to_all x1, blocking collectives, body(): full = lax.all_to_all(lifted(by_y.reshape(64, LINE)), 'x', 0, 0, tiled=True)  30 us
    all_to_all x1, blocking collectives, body(): by_y = lax.all_to_all(lines, 'y', 0, 0, tiled=True)  22.7 us
    all_to_all x1, waiting for transfers between devices, body(): lax.all_to_all(regrouped(w).reshape(N_K, N_F * C, WIDE), ('y', 'x'), 0, 0...  20 us
    all_to_all x1, starting transfers between devices, body(): lax.all_to_all(regrouped(w).reshape(N_K, N_F * C, WIDE), ('y', 'x'), 0, 0...  16.7 us
    pallas_call x1, Pallas kernels, finished(): pl.pallas_call(finish, grid=(LAYERS, N_X), in_specs=[pl.BlockSpec((1, 1,...  5.69 us
    pallas_call x1, Pallas kernels, regrouped(): pl.pallas_call(regroup, grid=(N_X,), in_specs=[whole(order.shape), pl.Blo...  3.92 us
  transfers between devices with their start and end apart: 1, of which 1 were waited for; matrix products, arithmetic and copies ran while one was open for 1% of the time, Pallas kernels for 0%

profile of v2, /device:TPU:6, one launch (start us, length us, event | category | flops | bytes accessed | tf_op | source)
XLA Modules:
  0.0 151.2 jit_solution(5435463910142679146)
XLA Ops:
  0.6 0.0 copy-start.2
  0.6 0.0 copy-start.1
  0.7 3.9 %regroup.1 = bf16[8,4,32,512]{3,2,1,0:T(8,128)(2,1)} custom-call(bf16[256,256]{1,0:T(8,128)(2,1)} %constant.57.clone.order_ref, bf16[16,4,16,512]{3,2,1,0:T(8,128)(2,1)} %bitcast.9), custom_call_target="tpu_custom_call" | custom-call | tf_op jit(solution)/shard_map/regroup/pallas_call | solution.py:102
  4.6 16.7 %all-to-all-start = ((bf16[32,32,512]{2,1,0:T(8,128)(2,1)}), bf16[32,32,512]{2,1,0:T(8,128)(2,1)S(1)}, u32[]{:S(2)}, u32[]{:S(2)}) async-start(bf16[32,32,512]{2,1,0:T(8,128)(2,1)} %bitcast.7), calls=%async_computation | async-start | bytes 2097152 | tf_op jit(solution)/shard_map/all_to_all | solution.py:166
  21.3 0.0 copy-done.2
  21.3 0.6 fusion
  21.9 0.0 copy-done.1
  21.9 0.9 add_convert_fusion.centered_ref
  22.8 20.0 %all-to-all-done.got_ref = bf16[32,32,512]{2,1,0:T(8,128)(2,1)S(1)} async-done(((bf16[32,32,512]{2,1,0:T(8,128)(2,1)}), bf16[32,32,512]{2,1,0:T(8,128)(2,1)S(1)}, u32[]{:S(2)}, u32[]{:S(2)}) %all-to-all-start) | async-done | bytes 1048608 | tf_op jit(solution)/shard_map/all_to_all | solution.py:166
  42.8 0.0 copy-start
  42.8 1.0 copy-done
  43.8 2.4 %pick.1 = bf16[2,128,512]{2,1,0:T(8,128)(2,1)} custom-call(s32[2]{0:T(128)} %get-tuple-element.6.owner_ref, bf16[128,128]{1,0:T(8,128)(2,1)} %constant.58.clone.order_ref, bf16[32,32,512]{2,1,0:T(8,128)(2,1)} %copy-done, bf16[512,512]{1,0:T(8,128)(2,1)} %add_convert_fusion.centered_ref), custom_call_target="tpu_custom_call" | custom-call | tf_op jit(solution)/shard_map/pick/pallas_call | solution.py:115
  46.3 41.9 %all_to_all.20 = bf16[32,8,512]{2,1,0:T(8,128)(2,1)} all-to-all(bf16[32,8,512]{2,1,0:T(8,128)(2,1)} %bitcast.10), channel_id=1, replica_groups=mesh['zl'=8,'co'=2,'y'=8,'zh'=2,'x'=4] {'zh','zl','co'}, dimensions={0} | all-to-all | bytes 524288 | tf_op jit(solution)/shard_map/all_to_all | solution.py:173
  88.2 2.0 %settle.1 = bf16[8,8,4352]{2,1,0:T(8,128)(2,1)} custom-call(s32[2]{0:T(128)} %get-tuple-element.7.half_ref, bf16[256,512]{1,0:T(8,128)(2,1)} %bitcast.11), custom_call_target="tpu_custom_call" | custom-call | tf_op jit(solution)/shard_map/settle/pallas_call | solution.py:125
  90.2 22.7 %all_to_all.21 = bf16[8,8,4352]{2,1,0:T(8,128)(2,1)} all-to-all(bf16[8,8,4352]{2,1,0:T(8,128)(2,1)} %settle.1), channel_id=1, replica_groups=mesh['zl'=8,'co'=2,'y'=8,'zh'=2,'x'=4] {'y'}, dimensions={0} | all-to-all | bytes 1114112 | tf_op jit(solution)/shard_map/all_to_all | solution.py:177
  112.8 2.7 %lift.1 = bf16[4,2,16,8704]{3,2,1,0:T(8,128)(2,1)} custom-call(bf16[64,64]{1,0:T(8,128)(2,1)} %constant.59.clone.order_ref, bf16[64,4352]{1,0:T(8,128)(2,1)} %bitcast.8), custom_call_target="tpu_custom_call" | custom-call | tf_op jit(solution)/shard_map/lift/pallas_call | solution.py:137
  115.6 30.0 %all_to_all.22.full_ref = bf16[4,2,16,8704]{3,2,1,0:T(8,128)(2,1)} all-to-all(bf16[4,2,16,8704]{3,2,1,0:T(8,128)(2,1)} %lift.1), channel_id=1, replica_groups=mesh['zl'=8,'co'=2,'y'=8,'zh'=2,'x'=4] {'x'}, dimensions={0} | all-to-all | bytes 4456448 | tf_op jit(solution)/shard_map/all_to_all | solution.py:178
  145.5 5.7 %finish.1 = (bf16[2,64,8192]{2,1,0:T(8,128)(2,1)}, bf16[2,64,512]{2,1,0:T(8,128)(2,1)}) custom-call(bf16[4,2,16,8704]{3,2,1,0:T(8,128)(2,1)} %all_to_all.22.full_ref), custom_call_target="tpu_custom_call" | custom-call | tf_op jit(solution)/shard_map/finish/pallas_call | solution.py:147
Async XLA Ops:
  0.6 20.7 %copy-start.2 = (s32[2]{0:T(128)S(1)}, s32[2]{0:T(128)}, u32[]{:S(2)}) copy-start(s32[2]{0:T(128)} %param.8) | copy-start | bytes 28
  0.6 21.2 %copy-start.1 = (s32[512,512]{1,0:T(8,128)S(1)}, s32[512,512]{1,0:T(8,128)}, u32[]{:S(2)}) copy-start(s32[512,512]{1,0:T(8,128)} %param.7) | copy-start | bytes 3145732
  4.6 38.3 %all-to-all-start = ((bf16[32,32,512]{2,1,0:T(8,128)(2,1)}), bf16[32,32,512]{2,1,0:T(8,128)(2,1)S(1)}, u32[]{:S(2)}, u32[]{:S(2)}) async-start(bf16[32,32,512]{2,1,0:T(8,128)(2,1)} %bitcast.7), calls=%async_computation | async-start | bytes 2097152 | tf_op jit(solution)/shard_map/all_to_all | solution.py:166
  42.8 1.0 copy-start

commit v3 on v2

--- a/solution.py
+++ b/solution.py
@@ -28,9 +28,10 @@
 
 
 def regroup(order_ref, w_ref, out_ref):
-    flat = w_ref[...].reshape(N_F * TALL, WIDE)
-    moved = jnp.dot(order_ref[...], flat, preferred_element_type=jnp.float32)
-    out_ref[...] = moved.astype(jnp.bfloat16).reshape(out_ref.shape)
+    for x in range(N_X):
+        flat = w_ref[:, x].reshape(N_F * TALL, WIDE)
+        moved = jnp.dot(order_ref[...], flat, preferred_element_type=jnp.float32)
+        out_ref[:, x] = moved.astype(jnp.bfloat16).reshape(N_Y, N_F * C, WIDE)
 
 
 def pick(owner_ref, order_ref, got_ref, centered_ref, out_ref):
@@ -79,13 +80,20 @@
                     out_ref[x, l, :, at : at + 256] = moved[r : r + TALL]
 
 
-def finish(full_ref, w_ref, f_ref):
-    w_ref[0] = full_ref[0, 0, :, :D]
-    f_ref[0] = full_ref[0, 0, :, D:]
-
-
-def whole(shape):
-    return pl.BlockSpec(shape, lambda *_: (0,) * len(shape))
+def finish(full_ref, w_ref, f_ref, done_ref):
+    copies = []
+    for l in range(LAYERS):
+        for x in range(N_X):
+            rows = pl.ds(x * TALL, TALL)
+            for part, (ref, columns) in enumerate(((w_ref, pl.ds(0, D)), (f_ref, pl.ds(D, FP)))):
+                copies.append(
+                    pltpu.make_async_copy(
+                        full_ref.at[x, l, :, columns], ref.at[l, rows, :], done_ref.at[l, x, part]
+                    )
+                )
+                copies[-1].start()
+    for copy in copies:
+        copy.wait()
 
 
 def shape_of(*dims):
@@ -101,11 +109,11 @@
     order = selection(spot // C % N_F * TALL + spot // (N_F * C) * C + spot % C, N_F * TALL)
     return pl.pallas_call(
         regroup,
-        grid=(N_X,),
-        in_specs=[whole(order.shape), pl.BlockSpec((N_F, 1, TALL, WIDE), lambda x: (0, x, 0, 0))],
-        out_specs=pl.BlockSpec((N_Y, 1, N_F * C, WIDE), lambda x: (0, x, 0, 0)),
+        in_specs=[VMEM, VMEM],
+        out_specs=VMEM,
         out_shape=shape_of(N_Y, N_X, N_F * C, WIDE),
         name="regroup",
+        compiler_params=pltpu.CompilerParams(vmem_limit_bytes=8 * 2**20),
     )(order, w.reshape(N_F, N_X, TALL, WIDE))
 
 
@@ -118,6 +126,7 @@
         out_specs=VMEM,
         out_shape=shape_of(N_ZH, 128, WIDE),
         name="pick",
+        compiler_params=pltpu.CompilerParams(vmem_limit_bytes=8 * 2**20),
     )(owner_k, order, got, centered)
 
 
@@ -128,6 +137,7 @@
         out_specs=VMEM,
         out_shape=shape_of(N_Y, 8, LINE),
         name="settle",
+        compiler_params=pltpu.CompilerParams(vmem_limit_bytes=6 * 2**20),
     )(owner_zh, recv)
 
 
@@ -140,20 +150,19 @@
         out_specs=VMEM,
         out_shape=shape_of(N_X, LAYERS, TALL, D + FP),
         name="lift",
+        compiler_params=pltpu.CompilerParams(vmem_limit_bytes=8 * 2**20),
     )(order, line)
 
 
 def finished(full):
     return pl.pallas_call(
         finish,
-        grid=(LAYERS, N_X),
-        in_specs=[pl.BlockSpec((1, 1, TALL, D + FP), lambda l, x: (x, l, 0, 0))],
-        out_specs=[
-            pl.BlockSpec((1, TALL, D), lambda l, x: (l, x, 0)),
-            pl.BlockSpec((1, TALL, FP), lambda l, x: (l, x, 0)),
-        ],
+        in_specs=[VMEM],
+        out_specs=[pl.BlockSpec(memory_space=pltpu.HBM)] * 2,
         out_shape=[shape_of(LAYERS, ROWS, D), shape_of(LAYERS, ROWS, FP)],
+        scratch_shapes=[pltpu.SemaphoreType.DMA((LAYERS, N_X, 2))],
         name="finish",
+        compiler_params=pltpu.CompilerParams(vmem_limit_bytes=8 * 2**20),
     )(full)
 
 

time: 153 us -> 139 us (0.908)
  Pallas kernels: 16.8 us -> 4.82 us
  blocking collectives: 94.6 us -> 92 us
    pallas_call x2, Pallas kernels: 9.61 us -> 2.89 us  [the longest x1 1.48 us: finished(): pl.pallas_call(finish, in_specs=[VMEM], out_specs=[pl.BlockSpec(memory_sp...]
    pallas_call x1, Pallas kernels: 2.74 us -> 0.29 us  [lifted(): pl.pallas_call(lift, in_specs=[VMEM, VMEM], out_specs=VMEM, out_shape=sha...]
    all_to_all x1, blocking collectives: 22.7 us -> 20.9 us  [body(): by_y = lax.all_to_all(lines, 'y', 0, 0, tiled=True)]
    pallas_call x1, Pallas kernels: 2.45 us -> 0.9 us  [picked(): pl.pallas_call(pick, in_specs=[SMEM, VMEM, VMEM, VMEM], out_specs=VMEM, o...]
  transfers between devices with their start and end apart: 1 -> 1, of which waited for: 1 -> 1; matrix products, arithmetic and copies ran while one was open for 1% -> 0% of each run, Pallas kernels for 0% -> 0%
where the time goes in v3:
time: 139 us; the launch traced here: 138 us
  blocking collectives  92 us (66%)
  waiting for transfers between devices  21.4 us (15%)
  starting transfers between devices  16.8 us (12%)
  Pallas kernels  4.82 us (3%)
  local copies, waits for them, and re-layouts  2.15 us (2%)
    all_to_all x1, blocking collectives, body(): lax.all_to_all(send.reshape(N_ZH * N_F, 8, WIDE), ('zh', 'zl', 'co'), 0,...  41.6 us
    all_to_all x1, blocking collectives, body(): full = lax.all_to_all(lifted(by_y.reshape(64, LINE)), 'x', 0, 0, tiled=True)  29.5 us
    all_to_all x1, waiting for transfers between devices, body(): lax.all_to_all(regrouped(w).reshape(N_K, N_F * C, WIDE), ('y', 'x'), 0, 0...  21.4 us
    all_to_all x1, blocking collectives, body(): by_y = lax.all_to_all(lines, 'y', 0, 0, tiled=True)  20.9 us
    all_to_all x1, starting transfers between devices, body(): lax.all_to_all(regrouped(w).reshape(N_K, N_F * C, WIDE), ('y', 'x'), 0, 0...  16.8 us
  transfers between devices with their start and end apart: 1, of which 1 were waited for; matrix products, arithmetic and copies ran while one was open for 0% of the time, Pallas kernels for 0%

profile of v3, /device:TPU:6, one launch (start us, length us, event | category | flops | bytes accessed | tf_op | source)
XLA Modules:
  0.0 138.0 jit_solution(12016724284005756527)
XLA Ops:
  0.6 0.0 copy-start.5
  0.6 0.0 copy-start
  0.6 1.2 copy-done
  1.9 0.0 copy-start.1
  1.9 0.9 copy-done.1
  2.8 0.0 copy-start.4
  2.8 1.4 %regroup.1 = bf16[8,4,32,512]{3,2,1,0:T(8,128)(2,1)} custom-call(bf16[256,256]{1,0:T(8,128)(2,1)S(1)} %copy-done.1, bf16[16,4,16,512]{3,2,1,0:T(8,128)(2,1)S(1)} %bitcast.8), custom_call_target="tpu_custom_call" | custom-call | tf_op jit(solution)/shard_map/regroup/pallas_call | solution.py:110
  4.2 0.0 copy-start.2
  4.2 16.8 %all-to-all-start = ((bf16[32,32,512]{2,1,0:T(8,128)(2,1)}), bf16[32,32,512]{2,1,0:T(8,128)(2,1)S(1)}, u32[]{:S(2)}, u32[]{:S(2)}) async-start(bf16[32,32,512]{2,1,0:T(8,128)(2,1)} %bitcast.1), calls=%async_computation | async-start | bytes 2097152 | tf_op jit(solution)/shard_map/all_to_all | solution.py:175
  21.0 0.0 copy-done.5
  21.1 0.0 copy-done.4
  21.1 0.1 add_convert_fusion.centered_ref
  21.2 0.0 copy-start.3
  21.2 21.4 %all-to-all-done.got_ref = bf16[32,32,512]{2,1,0:T(8,128)(2,1)S(1)} async-done(((bf16[32,32,512]{2,1,0:T(8,128)(2,1)}), bf16[32,32,512]{2,1,0:T(8,128)(2,1)S(1)}, u32[]{:S(2)}, u32[]{:S(2)}) %all-to-all-start) | async-done | bytes 1048608 | tf_op jit(solution)/shard_map/all_to_all | solution.py:175
  42.6 0.0 copy-done.2
  42.6 0.9 pick.1
  43.5 41.6 %all_to_all.20 = bf16[32,8,512]{2,1,0:T(8,128)(2,1)S(1)} all-to-all(bf16[32,8,512]{2,1,0:T(8,128)(2,1)S(1)} %bitcast.9), channel_id=1, replica_groups=mesh['zl'=8,'co'=2,'y'=8,'zh'=2,'x'=4] {'zh','zl','co'}, dimensions={0} | all-to-all | bytes 524288 | tf_op jit(solution)/shard_map/all_to_all | solution.py:182
  85.1 0.7 settle.1
  85.9 20.9 %all_to_all.21 = bf16[8,8,4352]{2,1,0:T(8,128)(2,1)S(1)} all-to-all(bf16[8,8,4352]{2,1,0:T(8,128)(2,1)S(1)} %settle.1), channel_id=1, replica_groups=mesh['zl'=8,'co'=2,'y'=8,'zh'=2,'x'=4] {'y'}, dimensions={0} | all-to-all | bytes 1114112 | tf_op jit(solution)/shard_map/all_to_all | solution.py:186
  106.7 0.0 copy-done.3
  106.7 0.3 lift.1
  107.0 29.5 %all_to_all.22.full_ref = bf16[4,2,16,8704]{3,2,1,0:T(8,128)(2,1)S(1)} all-to-all(bf16[4,2,16,8704]{3,2,1,0:T(8,128)(2,1)S(1)} %lift.1), channel_id=1, replica_groups=mesh['zl'=8,'co'=2,'y'=8,'zh'=2,'x'=4] {'x'}, dimensions={0} | all-to-all | bytes 4456448 | tf_op jit(solution)/shard_map/all_to_all | solution.py:187
  136.6 1.5 %finish.1 = (bf16[2,64,8192]{2,1,0:T(8,128)(2,1)}, bf16[2,64,512]{2,1,0:T(8,128)(2,1)}) custom-call(bf16[4,2,16,8704]{3,2,1,0:T(8,128)(2,1)S(1)} %all_to_all.22.full_ref), custom_call_target="tpu_custom_call" | custom-call | tf_op jit(solution)/shard_map/finish/pallas_call | solution.py:158
  (1 shorter events, 0.0 us)
Async XLA Ops:
  0.6 20.4 %copy-start.5 = (s32[2]{0:T(128)S(1)}, s32[2]{0:T(128)}, u32[]{:S(2)}) copy-start(s32[2]{0:T(128)} %param.8) | copy-start | bytes 28
  0.6 1.2 copy-start
  1.9 0.9 copy-start.1
  2.8 18.3 %copy-start.4 = (s32[512,512]{1,0:T(8,128)S(1)}, s32[512,512]{1,0:T(8,128)}, u32[]{:S(2)}) copy-start(s32[512,512]{1,0:T(8,128)} %param.7) | copy-start | bytes 3145732
  4.2 38.4 %copy-start.2 = (bf16[128,128]{1,0:T(8,128)(2,1)S(1)}, bf16[128,128]{1,0:T(8,128)(2,1)}, u32[]{:S(2)}) copy-start(bf16[128,128]{1,0:T(8,128)(2,1)} %constant.58.clone.order_ref) | copy-start | bytes 98308
  4.2 38.4 %all-to-all-start = ((bf16[32,32,512]{2,1,0:T(8,128)(2,1)}), bf16[32,32,512]{2,1,0:T(8,128)(2,1)S(1)}, u32[]{:S(2)}, u32[]{:S(2)}) async-start(bf16[32,32,512]{2,1,0:T(8,128)(2,1)} %bitcast.1), calls=%async_computation | async-start | bytes 2097152 | tf_op jit(solution)/shard_map/all_to_all | solution.py:175
  21.2 85.5 %copy-start.3 = (bf16[64,64]{1,0:T(8,128)(2,1)S(1)}, bf16[64,64]{1,0:T(8,128)(2,1)}, u32[]{:S(2)}) copy-start(bf16[64,64]{1,0:T(8,128)(2,1)} %constant.59.clone.order_ref) | copy-start | bytes 24580

commit v4 on v3

v4 whole, which is shorter than its diff:
```python
import jax
import jax.numpy as jnp
import numpy as np
from jax import lax
from jax.experimental import pallas as pl
from jax.experimental.pallas import tpu as pltpu
from jax.sharding import Mesh, PartitionSpec as P

D = 8192
COLS = 1024
FP = 512
LAYERS = 2
N_Y, N_ZH, N_X = 8, 2, 4
N_ZL, N_CO = 8, 2
N_F = N_ZL * N_CO
N_K = N_Y * N_X
WIDE = D // N_F
ROWS = COLS // N_F
C = ROWS // N_K
TALL = N_Y * C
FIRST = 3 * WIDE
SECOND = WIDE + FP // 4

spread_inverse = 1.0 / 72.0


def selection(source, count):
    return (np.asarray(source)[:, None] == np.arange(count)[None, :]).astype(jnp.bfloat16)


def regroup(w_ref, out_ref):
    size = N_F * TALL
    row = lax.broadcasted_iota(jnp.int32, (size, size), 0)
    col = lax.broadcasted_iota(jnp.int32, (size, size), 1)
    source = row // C % N_F * TALL + row // (N_F * C) * C + row % C
    order = jnp.where(col == source, 1.0, 0.0).astype(jnp.bfloat16)
    for x in range(N_X):
        flat = w_ref[:, x].reshape(size, WIDE)
        moved = jnp.dot(order, flat, preferred_element_type=jnp.float32)
        out_ref[:, x] = moved.astype(jnp.bfloat16).reshape(N_Y, N_F * C, WIDE)


def pick(owner_ref, order_ref, got_ref, centered_ref, out_ref):
    chosen = jnp.concatenate([got_ref[owner_ref[0]], got_ref[owner_ref[1]]], axis=0)
    part = jnp.dot(chosen, centered_ref[...], preferred_element_type=jnp.float32)
    both = jnp.concatenate([chosen, part.astype(jnp.bfloat16)], axis=0)
    moved = jnp.dot(order_ref[...], both, preferred_element_type=jnp.float32).astype(jnp.bfloat16)
    for half in range(N_ZH):
        out_ref[half] = moved


def settle(half_ref, recv_ref, *out_refs):
    recv = recv_ref[...]
    row = lax.broadcasted_iota(jnp.int32, (64, 256), 0)
    col = lax.broadcasted_iota(jnp.int32, (64, 256), 1)
    layer = row // 32
    z_hi = jnp.where(layer == 0, half_ref[0], half_ref[1])
    source = z_hi * 128 + (row // 2 % 4 * 4 + row // 8 % 4) * 8 + layer * C + row % 2
    weights = jnp.dot(
        jnp.where(col == source, 1.0, 0.0).astype(jnp.bfloat16), recv,
        preferred_element_type=jnp.float32,
    )
    row, col = row[:16], col[:16]
    layer = row // 8
    z_hi = jnp.where(layer == 0, half_ref[0], half_ref[1])
    hit = (col // 128 == z_hi) & (col % 8 == 4 + layer * C + row % 2)
    summed = jnp.dot(
        jnp.where(hit, 1.0, 0.0).astype(jnp.bfloat16), recv, preferred_element_type=jnp.float32
    ) * spread_inverse
    quarter = lax.broadcasted_iota(jnp.int32, (16, 128), 0) // 2 % 4
    prints = summed[:, :128]
    for q in range(1, 4):
        prints = jnp.where(quarter == q, summed[:, 128 * q : 128 * q + 128], prints)
    first_ref, second_ref = out_refs
    for l in range(LAYERS):
        for low in range(4):
            r = 32 * l + 8 * low
            moved = weights[r : r + 8].astype(jnp.bfloat16)
            if low == 3:
                second_ref[l, :, :WIDE] = moved
            else:
                for y in range(N_Y):
                    first_ref[y, l, :, WIDE * low : WIDE * (low + 1)] = moved
        second_ref[l, :, WIDE:] = prints[8 * l : 8 * l + 8].astype(jnp.bfloat16)


def fan(*refs):
    for y in range(N_Y):
        for i in range(N_X):
            refs[-1][y, i] = refs[i][...]


def lift(order_ref, line_ref, *out_refs):
    for at in range(0, FIRST, 256):
        moved = jnp.dot(
            order_ref[...], line_ref[:, at : at + 256], preferred_element_type=jnp.float32
        ).astype(jnp.bfloat16)
        for l in range(LAYERS):
            for q in range(4):
                r = 64 * l + TALL * q
                out_refs[l][:, FIRST * q + at : FIRST * q + at + 256] = moved[r : r + TALL]


def lift_rest(order_ref, line_ref, w_ref, f_ref):
    for l in range(LAYERS):
        for i in range(N_X):
            moved = jnp.dot(
                order_ref[...], line_ref[:, i, l].reshape(64, SECOND), preferred_element_type=jnp.float32
            ).astype(jnp.bfloat16)
            for q in range(4):
                part = moved[TALL * q : TALL * q + TALL]
                w_ref[l, i, :, WIDE * q : WIDE * q + WIDE] = part[:, :WIDE]
                f_ref[l, i, :, 128 * q : 128 * q + 128] = part[:, WIDE:]


def finish(me_ref, *refs):
    slabs, (rest_ref, prints_ref, w_ref, f_ref, done_ref) = refs[: LAYERS * N_X], refs[LAYERS * N_X :]
    me = me_ref[0]
    copies = []

    def send(source, target, done):
        copies.append(pltpu.make_async_copy(source, target, done))
        copies[-1].start()

    for l in range(LAYERS):
        for i, step in enumerate((0, 3, 1, 2)):
            rows = pl.ds(pl.multiple_of((me + step) % N_X * TALL, TALL), TALL)
            for q in range(4):
                at = D // 4 * q
                send(
                    slabs[l * N_X + i].at[:, pl.ds(FIRST * q, FIRST)],
                    w_ref.at[l, rows, pl.ds(at, FIRST)], done_ref.at[l, i, q],
                )
                send(
                    rest_ref.at[l, i, :, pl.ds(WIDE * q, WIDE)],
                    w_ref.at[l, rows, pl.ds(at + FIRST, WIDE)], done_ref.at[l, i, 4 + q],
                )
            send(prints_ref.at[l, i], f_ref.at[l, rows, :], done_ref.at[l, i, 8])
    for copy in copies:
        copy.wait()


def shape_of(*dims):
    return jax.ShapeDtypeStruct(dims, jnp.bfloat16)


VMEM = pl.BlockSpec(memory_space=pltpu.VMEM)
SMEM = pl.BlockSpec(memory_space=pltpu.SMEM)


def regrouped(w):
    return pl.pallas_call(
        regroup,
        in_specs=[VMEM],
        out_specs=VMEM,
        out_shape=shape_of(N_Y, N_X, N_F * C, WIDE),
        name="regroup",
        compiler_params=pltpu.CompilerParams(vmem_limit_bytes=8 * 2**20),
    )(w.reshape(N_F, N_X, TALL, WIDE))


def picked(owner_k, got, centered):
    spot = np.arange(128)
    order = selection(spot // 4 % 2 * 64 + spot // 2 % 2 * 32 + spot // 8 * 2 + spot % 2, 128)
    return pl.pallas_call(
        pick,
        in_specs=[SMEM, VMEM, VMEM, VMEM],
        out_specs=VMEM,
        out_shape=shape_of(N_ZH, 128, WIDE),
        name="pick",
        compiler_params=pltpu.CompilerParams(vmem_limit_bytes=8 * 2**20),
    )(owner_k, order, got, centered)


def settled(owner_zh, recv):
    return pl.pallas_call(
        settle,
        in_specs=[SMEM, VMEM],
        out_specs=[VMEM] * 2,
        out_shape=[shape_of(N_Y, LAYERS, 8, FIRST), shape_of(LAYERS, 8, SECOND)],
        name="settle",
        compiler_params=pltpu.CompilerParams(vmem_limit_bytes=6 * 2**20),
    )(owner_zh, recv)


def fanned(parts):
    return pl.pallas_call(
        fan,
        in_specs=[VMEM] * N_X,
        out_specs=VMEM,
        out_shape=shape_of(N_Y, N_X, LAYERS, 8, SECOND),
        name="fan",
        compiler_params=pltpu.CompilerParams(vmem_limit_bytes=6 * 2**20),
    )(*parts)


def lifted(line):
    spot = np.arange(128)
    order = selection(spot // 2 % 8 * 16 + spot // 64 * 8 + spot // 16 % 4 * 2 + spot % 2, 128)
    return pl.pallas_call(
        lift,
        in_specs=[VMEM, VMEM],
        out_specs=[VMEM] * LAYERS,
        out_shape=[shape_of(TALL, 4 * FIRST)] * LAYERS,
        name="lift",
        compiler_params=pltpu.CompilerParams(vmem_limit_bytes=6 * 2**20),
    )(order, line)


def lifted_rest(line):
    spot = np.arange(64)
    order = selection(spot // 2 % 8 * 8 + spot // 16 * 2 + spot % 2, 64)
    return pl.pallas_call(
        lift_rest,
        in_specs=[VMEM, VMEM],
        out_specs=[VMEM] * 2,
        out_shape=[shape_of(LAYERS, N_X, TALL, 4 * WIDE), shape_of(LAYERS, N_X, TALL, FP)],
        name="lift_rest",
        compiler_params=pltpu.CompilerParams(vmem_limit_bytes=6 * 2**20),
    )(order, line)


def finished(me, slabs):
    return pl.pallas_call(
        finish,
        in_specs=[SMEM] + [VMEM] * (LAYERS * N_X + 2),
        out_specs=[pl.BlockSpec(memory_space=pltpu.HBM)] * 2,
        out_shape=[shape_of(LAYERS, ROWS, D), shape_of(LAYERS, ROWS, FP)],
        scratch_shapes=[pltpu.SemaphoreType.DMA((LAYERS, N_X, 9))],
        name="finish",
        compiler_params=pltpu.CompilerParams(vmem_limit_bytes=8 * 2**20),
    )(me, *slabs)


def solution(mesh):
    fine = Mesh(
        mesh.devices.reshape(N_ZL, N_CO, N_Y, N_ZH, N_X), ("zl", "co", "y", "zh", "x")
    )

    def body(w, table, assign):
        got = lax.all_to_all(
            regrouped(w).reshape(N_K, N_F * C, WIDE), ("y", "x"), 0, 0, tiled=True
        )
        centered = (table - 125).astype(jnp.bfloat16)
        owner_zh = assign // N_X % N_ZH
        owner_k = assign // (N_ZH * N_X) * N_X + assign % N_X
        send = picked(owner_k, got, centered)
        recv = lax.all_to_all(
            send.reshape(N_ZH * N_F, 8, WIDE), ("zh", "zl", "co"), 0, 0, tiled=True
        )
        first, second = settled(owner_zh, recv.reshape(N_ZH * 128, WIDE))
        right = [(i, (i + 1) % N_X) for i in range(N_X)]
        left = [(i, (i - 1) % N_X) for i in range(N_X)]
        across = [(i, (i + 2) % N_X) for i in range(N_X)]
        by_y = lax.all_to_all(first, "y", 0, 0, tiled=True)
        by_x = [second] + [lax.ppermute(second, "x", way) for way in (right, left, across)]
        own = lifted(by_y.reshape(N_Y * LAYERS * 8, FIRST))
        rest = lifted_rest(lax.all_to_all(fanned(by_x), "y", 0, 0, tiled=True))
        before = [lax.ppermute(v, "x", right) for v in own]
        after = [lax.ppermute(v, "x", left) for v in own]
        far = [lax.ppermute(before[0], "x", right), lax.ppermute(after[1], "x", left)]
        slabs = [v[l] for l in range(LAYERS) for v in (own, before, after, far)]
        w_out, f_out = finished(lax.axis_index("x").reshape(1), slabs + list(rest))
        return w_out[None], f_out[None]

    roll = ("y", "zh", "x")
    fsdp = ("zl", "co")
    return jax.shard_map(
        body, mesh=fine, in_specs=(P(roll, None, fsdp), P(fsdp, None), P(None)),
        out_specs=(P(roll, None, fsdp, None), P(roll, None, fsdp, None)), check_vma=False,
    )
```

time: 139 us -> 140 us (level)
  blocking collectives: 92 us -> 41.6 us
  starting transfers between devices: 16.8 us -> 56 us
  waiting for transfers between devices: 21.4 us -> 31.4 us
  Pallas kernels: 4.82 us -> 7.19 us
    all_to_all x2 -> x0, blocking collectives: 50.4 us -> none  [the longest x1 29.5 us: body(): full = lax.all_to_all(lifted(by_y.reshape(64, LINE)), 'x', 0, 0, tiled=True)]
    ppermute x0 -> x9, starting transfers between devices: none -> 30.7 us  [the longest x2 10.6 us: body(): before = [lax.ppermute(v, 'x', right) for v in own]]
    all_to_all x0 -> x2, starting transfers between devices: none -> 8.47 us  [the longest x1 5.02 us: body(): rest = lifted_rest(lax.all_to_all(fanned(by_x), 'y', 0, 0, tiled=True))]
    ppermute x0 -> x9, waiting for transfers between devices: none -> 7.93 us  [the longest x1 5.15 us: body(): lax.ppermute(after[1], 'x', left)]
    pallas_call x4 -> x6, Pallas kernels: 3.92 us -> 6.29 us  [the longest x1 1.96 us: finished(): pl.pallas_call(finish, in_specs=[SMEM] + [VMEM] * (LAYERS * N_X + 2), out...]
    all_to_all x0 -> x2, waiting for transfers between devices: none -> 2.1 us  [the longest x1 2.1 us: body(): by_y = lax.all_to_all(first, 'y', 0, 0, tiled=True)]
  transfers between devices with their start and end apart: 1 -> 12, of which waited for: 1 -> 5; matrix products, arithmetic and copies ran while one was open for 0% -> 0% of each run, Pallas kernels for 0% -> 1%
where the time goes in v4:
time: 140 us; the launch traced here: 138 us
  starting transfers between devices  56 us (40%)
  blocking collectives  41.6 us (30%)
  waiting for transfers between devices  31.4 us (22%)
  Pallas kernels  7.19 us (5%)
    all_to_all x1, blocking collectives, body(): lax.all_to_all(send.reshape(N_ZH * N_F, 8, WIDE), ('zh', 'zl', 'co'), 0,...  41.6 us
    all_to_all x1, waiting for transfers between devices, body(): lax.all_to_all(regrouped(w).reshape(N_K, N_F * C, WIDE), ('y', 'x'), 0, 0...  21.4 us
    all_to_all x1, starting transfers between devices, body(): lax.all_to_all(regrouped(w).reshape(N_K, N_F * C, WIDE), ('y', 'x'), 0, 0...  16.8 us
    ppermute x2, starting transfers between devices, body(): before = [lax.ppermute(v, 'x', right) for v in own]  10.6 us
    ppermute x3, starting transfers between devices, body(): lax.ppermute(second, 'x', way)  10.4 us
    ppermute x1, waiting for transfers between devices, body(): lax.ppermute(after[1], 'x', left)  5.15 us
    all_to_all x1, starting transfers between devices, body(): rest = lifted_rest(lax.all_to_all(fanned(by_x), 'y', 0, 0, tiled=True))  5.02 us
    ppermute x1, starting transfers between devices, body(): lax.ppermute(before[0], 'x', right)  3.92 us
  transfers between devices with their start and end apart: 12, of which 5 were waited for; matrix products, arithmetic and copies ran while one was open for 0% of the time, Pallas kernels for 1%

profile of v4, /device:TPU:6, one launch (start us, length us, event | category | flops | bytes accessed | tf_op | source)
XLA Modules:
  0.0 138.5 jit_solution(17485418404322250554)
XLA Ops:
  0.6 1.2 copy-done
  1.9 1.4 %regroup.1 = bf16[8,4,32,512]{3,2,1,0:T(8,128)(2,1)} custom-call(bf16[16,4,16,512]{3,2,1,0:T(8,128)(2,1)S(1)} %bitcast.9), custom_call_target="tpu_custom_call" | custom-call | tf_op jit(solution)/shard_map/regroup/pallas_call | solution.py:152
  3.3 16.8 %all-to-all-start = ((bf16[32,32,512]{2,1,0:T(8,128)(2,1)}), bf16[32,32,512]{2,1,0:T(8,128)(2,1)S(1)}, u32[]{:S(2)}, u32[]{:S(2)}) async-start(bf16[32,32,512]{2,1,0:T(8,128)(2,1)} %bitcast.2), calls=%async_computation | async-start | bytes 2097152 | tf_op jit(solution)/shard_map/all_to_all | solution.py:241
  20.2 0.1 add_convert_fusion.centered_ref
  20.3 21.4 %all-to-all-done.got_ref = bf16[32,32,512]{2,1,0:T(8,128)(2,1)S(1)} async-done(((bf16[32,32,512]{2,1,0:T(8,128)(2,1)}), bf16[32,32,512]{2,1,0:T(8,128)(2,1)S(1)}, u32[]{:S(2)}, u32[]{:S(2)}) %all-to-all-start) | async-done | bytes 1048608 | tf_op jit(solution)/shard_map/all_to_all | solution.py:241
  41.7 0.9 pick.1
  42.6 0.0 copy-start.2
  42.6 0.0 copy-start.3
  42.6 41.6 %all_to_all.20 = bf16[32,8,512]{2,1,0:T(8,128)(2,1)S(1)} all-to-all(bf16[32,8,512]{2,1,0:T(8,128)(2,1)S(1)} %bitcast.11), channel_id=1, replica_groups=mesh['zl'=8,'co'=2,'y'=8,'zh'=2,'x'=4] {'zh','zl','co'}, dimensions={0} | all-to-all | bytes 524288 | tf_op jit(solution)/shard_map/all_to_all | solution.py:248
  84.2 1.5 %settle.1 = (bf16[8,2,8,1536]{3,2,1,0:T(8,128)(2,1)}, bf16[2,8,640]{2,1,0:T(8,128)(2,1)S(1)}) custom-call(s32[2]{0:T(128)S(1)} %get-tuple-element.19.half_ref, bf16[256,512]{1,0:T(8,128)(2,1)S(1)} %bitcast.10), custom_call_target="tpu_custom_call" | custom-call | tf_op jit(solution)/shard_map/settle/pallas_call | solution.py:176
  85.7 3.5 %all-to-all-start.2 = ((bf16[8,2,8,1536]{3,2,1,0:T(8,128)(2,1)}), bf16[8,2,8,1536]{3,2,1,0:T(8,128)(2,1)S(1)}, u32[]{:S(2)}, u32[]{:S(2)}) async-start(bf16[8,2,8,1536]{3,2,1,0:T(8,128)(2,1)} %get-tuple-element.10), calls=%async_computation.2 | async-start | bytes 786432 | tf_op jit(solution)/shard_map/all_to_all | solution.py:255
  89.2 3.4 %collective-permute-start.8 = (bf16[2,8,640]{2,1,0:T(8,128)(2,1)S(1)}, bf16[2,8,640]{2,1,0:T(8,128)(2,1)S(1)}, u32[]{:S(2)}, u32[]{:S(2)}) collective-permute-start(bf16[2,8,640]{2,1,0:T(8,128)(2,1)S(1)} %get-tuple-element.13.refs_0_), channel_id=1, source_target_pairs={{0,2},{1,3},{2,0},{3,1},{4,6},{5,7},{6,4},{7,5},{8,10},{9,11},{10,... | collective-permute-start | bytes 61448 | tf_op jit(solution)/shard_map/ppermute | solution.py:256
  92.5 2.2 %collective-permute-start.7 = (bf16[2,8,640]{2,1,0:T(8,128)(2,1)S(1)}, bf16[2,8,640]{2,1,0:T(8,128)(2,1)S(1)}, u32[]{:S(2)}, u32[]{:S(2)}) collective-permute-start(bf16[2,8,640]{2,1,0:T(8,128)(2,1)S(1)} %get-tuple-element.13.refs_0_), channel_id=1, source_target_pairs={{0,3},{1,0},{2,1},{3,2},{4,7},{5,4},{6,5},{7,6},{8,11},{9,8},{10,9... | collective-permute-start | bytes 61448 | tf_op jit(solution)/shard_map/ppermute | solution.py:256
  94.7 4.9 %collective-permute-start.6 = (bf16[2,8,640]{2,1,0:T(8,128)(2,1)S(1)}, bf16[2,8,640]{2,1,0:T(8,128)(2,1)S(1)}, u32[]{:S(2)}, u32[]{:S(2)}) collective-permute-start(bf16[2,8,640]{2,1,0:T(8,128)(2,1)S(1)} %get-tuple-element.13.refs_0_), channel_id=1, source_target_pairs={{0,1},{1,2},{2,3},{3,0},{4,5},{5,6},{6,7},{7,4},{8,9},{9,10},{10,1... | collective-permute-start | bytes 61448 | tf_op jit(solution)/shard_map/ppermute | solution.py:256
  99.6 0.0 collective-permute-done.7.refs_2_
  99.6 1.4 %collective-permute-done.6.refs_1_ = bf16[2,8,640]{2,1,0:T(8,128)(2,1)S(1)} collective-permute-done((bf16[2,8,640]{2,1,0:T(8,128)(2,1)S(1)}, bf16[2,8,640]{2,1,0:T(8,128)(2,1)S(1)}, u32[]{:S(2)}, u32[]{:S(2)}) %collective-permute-start.6) | collective-permute-done | bytes 20512 | tf_op jit(solution)/shard_map/ppermute | solution.py:256
  101.1 0.9 fan.1
  102.0 2.1 %all-to-all-done.2 = bf16[8,2,8,1536]{3,2,1,0:T(8,128)(2,1)S(1)} async-done(((bf16[8,2,8,1536]{3,2,1,0:T(8,128)(2,1)}), bf16[8,2,8,1536]{3,2,1,0:T(8,128)(2,1)S(1)}, u32[]{:S(2)}, u32[]{:S(2)}) %all-to-all-start.2) | async-done | bytes 393248 | tf_op jit(solution)/shard_map/all_to_all | solution.py:255
  104.1 5.0 %all-to-all-start.3 = ((bf16[8,4,2,8,640]{4,3,2,1,0:T(8,128)(2,1)}), bf16[8,4,2,8,640]{4,3,2,1,0:T(8,128)(2,1)S(1)}, u32[]{:S(2)}, u32[]{:S(2)}) async-start(bf16[8,4,2,8,640]{4,3,2,1,0:T(8,128)(2,1)} %fan.1), calls=%async_computation.3 | async-start | bytes 1310720 | tf_op jit(solution)/shard_map/all_to_all | solution.py:258
  109.1 0.2 lift.1
  109.3 5.4 %collective-permute-start = (bf16[16,6144]{1,0:T(8,128)(2,1)S(1)}, bf16[16,6144]{1,0:T(8,128)(2,1)S(1)}, u32[]{:S(2)}, u32[]{:S(2)}) collective-permute-start(bf16[16,6144]{1,0:T(8,128)(2,1)S(1)} %get-tuple-element.11.refs_0_), channel_id=1, source_target_pairs={{0,1},{1,2},{2,3},{3,0},{4,5},{5,6},{6,7},{7,4},{8,9},{9,10},{10,1... | collective-permute-start | bytes 589832 | tf_op jit(solution)/shard_map/ppermute | solution.py:259
  114.8 1.9 %collective-permute-start.4 = (bf16[16,6144]{1,0:T(8,128)(2,1)S(1)}, bf16[16,6144]{1,0:T(8,128)(2,1)S(1)}, u32[]{:S(2)}, u32[]{:S(2)}) collective-permute-start(bf16[16,6144]{1,0:T(8,128)(2,1)S(1)} %get-tuple-element.12.refs_4_), channel_id=1, source_target_pairs={{0,3},{1,0},{2,1},{3,2},{4,7},{5,4},{6,5},{7,6},{8,11},{9,8},{10,9... | collective-permute-start | bytes 589832 | tf_op jit(solution)/shard_map/ppermute | solution.py:260
  116.7 1.9 %collective-permute-start.1 = (bf16[16,6144]{1,0:T(8,128)(2,1)S(1)}, bf16[16,6144]{1,0:T(8,128)(2,1)S(1)}, u32[]{:S(2)}, u32[]{:S(2)}) collective-permute-start(bf16[16,6144]{1,0:T(8,128)(2,1)S(1)} %get-tuple-element.11.refs_0_), channel_id=1, source_target_pairs={{0,3},{1,0},{2,1},{3,2},{4,7},{5,4},{6,5},{7,6},{8,11},{9,8},{10,9... | collective-permute-start | bytes 589832 | tf_op jit(solution)/shard_map/ppermute | solution.py:260
  118.6 5.1 %collective-permute-start.3 = (bf16[16,6144]{1,0:T(8,128)(2,1)S(1)}, bf16[16,6144]{1,0:T(8,128)(2,1)S(1)}, u32[]{:S(2)}, u32[]{:S(2)}) collective-permute-start(bf16[16,6144]{1,0:T(8,128)(2,1)S(1)} %get-tuple-element.12.refs_4_), channel_id=1, source_target_pairs={{0,1},{1,2},{2,3},{3,0},{4,5},{5,6},{6,7},{7,4},{8,9},{9,10},{10,1... | collective-permute-start | bytes 589832 | tf_op jit(solution)/shard_map/ppermute | solution.py:259
  123.8 0.0 collective-permute-done.refs_1_
  123.8 3.9 %collective-permute-start.2 = (bf16[16,6144]{1,0:T(8,128)(2,1)S(1)}, bf16[16,6144]{1,0:T(8,128)(2,1)S(1)}, u32[]{:S(2)}, u32[]{:S(2)}) collective-permute-start(bf16[16,6144]{1,0:T(8,128)(2,1)S(1)} %collective-permute-done.refs_1_), channel_id=1, source_target_pairs={{0,1},{1,2},{2,3},{3,0},{4,5},{5,6},{6,7},{7,4},{8,9},{9,10},{10,1... | collective-permute-start | bytes 589832 | tf_op jit(solution)/shard_map/ppermute | solution.py:261
  127.7 0.0 collective-permute-done.4.refs_6_
  127.7 1.9 %collective-permute-start.5 = (bf16[16,6144]{1,0:T(8,128)(2,1)S(1)}, bf16[16,6144]{1,0:T(8,128)(2,1)S(1)}, u32[]{:S(2)}, u32[]{:S(2)}) collective-permute-start(bf16[16,6144]{1,0:T(8,128)(2,1)S(1)} %collective-permute-done.4.refs_6_), channel_id=1, source_target_pairs={{0,3},{1,0},{2,1},{3,2},{4,7},{5,4},{6,5},{7,6},{8,11},{9,8},{10,9... | collective-permute-start | bytes 589832 | tf_op jit(solution)/shard_map/ppermute | solution.py:261
  129.7 0.3 lift_rest.1
  130.0 1.3 collective-permute-done.2.refs_3_
  131.3 5.2 %collective-permute-done.5.refs_7_ = bf16[16,6144]{1,0:T(8,128)(2,1)S(1)} collective-permute-done((bf16[16,6144]{1,0:T(8,128)(2,1)S(1)}, bf16[16,6144]{1,0:T(8,128)(2,1)S(1)}, u32[]{:S(2)}, u32[]{:S(2)}) %collective-permute-start.5) | collective-permute-done | bytes 196640 | tf_op jit(solution)/shard_map/ppermute | solution.py:261
  136.5 2.0 %finish.1 = (bf16[2,64,8192]{2,1,0:T(8,128)(2,1)}, bf16[2,64,512]{2,1,0:T(8,128)(2,1)}) custom-call(s32[1]{0:T(128)} %bitcast.me_ref, bf16[16,6144]{1,0:T(8,128)(2,1)S(1)} %get-tuple-element.11.refs_0_, bf16[16,6144]{1,0:T(8,128)(2,1)S(1)} %collective-permute-done.refs_1_, bf16[16,6144]{1,0:T(8,128)(2,1)S(1)} %collective-permute-done.1.refs_2_, ...), custom_call_target="tpu_custom_call" | custom-call | tf_op jit(solution)/shard_map/finish/pallas_call | solution.py:224
  (14 shorter events, 0.0 us)
Async XLA Ops:
  0.6 1.2 copy-start
  1.9 18.3 %copy-start.5 = (s32[2]{0:T(128)S(1)}, s32[2]{0:T(128)}, u32[]{:S(2)}) copy-start(s32[2]{0:T(128)} %param.8) | copy-start | bytes 28
  1.9 18.3 %copy-start.4 = (s32[512,512]{1,0:T(8,128)S(1)}, s32[512,512]{1,0:T(8,128)}, u32[]{:S(2)}) copy-start(s32[512,512]{1,0:T(8,128)} %param.7) | copy-start | bytes 3145732
  3.3 38.4 %copy-start.1 = (bf16[128,128]{1,0:T(8,128)(2,1)S(1)}, bf16[128,128]{1,0:T(8,128)(2,1)}, u32[]{:S(2)}) copy-start(bf16[128,128]{1,0:T(8,128)(2,1)} %constant.61.clone.order_ref) | copy-start | bytes 98308
  3.3 38.4 %all-to-all-start = ((bf16[32,32,512]{2,1,0:T(8,128)(2,1)}), bf16[32,32,512]{2,1,0:T(8,128)(2,1)S(1)}, u32[]{:S(2)}, u32[]{:S(2)}) async-start(bf16[32,32,512]{2,1,0:T(8,128)(2,1)} %bitcast.2), calls=%async_computation | async-start | bytes 2097152 | tf_op jit(solution)/shard_map/all_to_all | solution.py:241
  42.6 66.5 %copy-start.2 = (bf16[128,128]{1,0:T(8,128)(2,1)S(1)}, bf16[128,128]{1,0:T(8,128)(2,1)}, u32[]{:S(2)}) copy-start(bf16[128,128]{1,0:T(8,128)(2,1)} %constant.62.clone.order_ref) | copy-start | bytes 98308
  42.6 87.1 %copy-start.3 = (bf16[64,64]{1,0:T(8,128)(2,1)S(1)}, bf16[64,64]{1,0:T(8,128)(2,1)}, u32[]{:S(2)}) copy-start(bf16[64,64]{1,0:T(8,128)(2,1)} %constant.63.clone.order_ref) | copy-start | bytes 24580
  85.7 18.4 %all-to-all-start.2 = ((bf16[8,2,8,1536]{3,2,1,0:T(8,128)(2,1)}), bf16[8,2,8,1536]{3,2,1,0:T(8,128)(2,1)S(1)}, u32[]{:S(2)}, u32[]{:S(2)}) async-start(bf16[8,2,8,1536]{3,2,1,0:T(8,128)(2,1)} %get-tuple-element.10), calls=%async_computation.2 | async-start | bytes 786432 | tf_op jit(solution)/shard_map/all_to_all | solution.py:255
  89.2 10.4 %collective-permute-start.8 = (bf16[2,8,640]{2,1,0:T(8,128)(2,1)S(1)}, bf16[2,8,640]{2,1,0:T(8,128)(2,1)S(1)}, u32[]{:S(2)}, u32[]{:S(2)}) collective-permute-start(bf16[2,8,640]{2,1,0:T(8,128)(2,1)S(1)} %get-tuple-element.13.refs_0_), channel_id=1, source_target_pairs={{0,2},{1,3},{2,0},{3,1},{4,6},{5,7},{6,4},{7,5},{8,10},{9,11},{10,... | collective-permute-start | bytes 61448 | tf_op jit(solution)/shard_map/ppermute | solution.py:256
  92.5 7.1 %collective-permute-start.7 = (bf16[2,8,640]{2,1,0:T(8,128)(2,1)S(1)}, bf16[2,8,640]{2,1,0:T(8,128)(2,1)S(1)}, u32[]{:S(2)}, u32[]{:S(2)}) collective-permute-start(bf16[2,8,640]{2,1,0:T(8,128)(2,1)S(1)} %get-tuple-element.13.refs_0_), channel_id=1, source_target_pairs={{0,3},{1,0},{2,1},{3,2},{4,7},{5,4},{6,5},{7,6},{8,11},{9,8},{10,9... | collective-permute-start | bytes 61448 | tf_op jit(solution)/shard_map/ppermute | solution.py:256
  94.7 6.4 %collective-permute-start.6 = (bf16[2,8,640]{2,1,0:T(8,128)(2,1)S(1)}, bf16[2,8,640]{2,1,0:T(8,128)(2,1)S(1)}, u32[]{:S(2)}, u32[]{:S(2)}) collective-permute-start(bf16[2,8,640]{2,1,0:T(8,128)(2,1)S(1)} %get-tuple-element.13.refs_0_), channel_id=1, source_target_pairs={{0,1},{1,2},{2,3},{3,0},{4,5},{5,6},{6,7},{7,4},{8,9},{9,10},{10,1... | collective-permute-start | bytes 61448 | tf_op jit(solution)/shard_map/ppermute | solution.py:256
  104.1 25.6 %all-to-all-start.3 = ((bf16[8,4,2,8,640]{4,3,2,1,0:T(8,128)(2,1)}), bf16[8,4,2,8,640]{4,3,2,1,0:T(8,128)(2,1)S(1)}, u32[]{:S(2)}, u32[]{:S(2)}) async-start(bf16[8,4,2,8,640]{4,3,2,1,0:T(8,128)(2,1)} %fan.1), calls=%async_computation.3 | async-start | bytes 1310720 | tf_op jit(solution)/shard_map/all_to_all | solution.py:258
  109.3 14.4 %collective-permute-start = (bf16[16,6144]{1,0:T(8,128)(2,1)S(1)}, bf16[16,6144]{1,0:T(8,128)(2,1)S(1)}, u32[]{:S(2)}, u32[]{:S(2)}) collective-permute-start(bf16[16,6144]{1,0:T(8,128)(2,1)S(1)} %get-tuple-element.11.refs_0_), channel_id=1, source_target_pairs={{0,1},{1,2},{2,3},{3,0},{4,5},{5,6},{6,7},{7,4},{8,9},{9,10},{10,1... | collective-permute-start | bytes 589832 | tf_op jit(solution)/shard_map/ppermute | solution.py:259
  114.8 12.9 %collective-permute-start.4 = (bf16[16,6144]{1,0:T(8,128)(2,1)S(1)}, bf16[16,6144]{1,0:T(8,128)(2,1)S(1)}, u32[]{:S(2)}, u32[]{:S(2)}) collective-permute-start(bf16[16,6144]{1,0:T(8,128)(2,1)S(1)} %get-tuple-element.12.refs_4_), channel_id=1, source_target_pairs={{0,3},{1,0},{2,1},{3,2},{4,7},{5,4},{6,5},{7,6},{8,11},{9,8},{10,9... | collective-permute-start | bytes 589832 | tf_op jit(solution)/shard_map/ppermute | solution.py:260
  116.7 13.3 %collective-permute-start.1 = (bf16[16,6144]{1,0:T(8,128)(2,1)S(1)}, bf16[16,6144]{1,0:T(8,128)(2,1)S(1)}, u32[]{:S(2)}, u32[]{:S(2)}) collective-permute-start(bf16[16,6144]{1,0:T(8,128)(2,1)S(1)} %get-tuple-element.11.refs_0_), channel_id=1, source_target_pairs={{0,3},{1,0},{2,1},{3,2},{4,7},{5,4},{6,5},{7,6},{8,11},{9,8},{10,9... | collective-permute-start | bytes 589832 | tf_op jit(solution)/shard_map/ppermute | solution.py:260
  118.6 11.4 %collective-permute-start.3 = (bf16[16,6144]{1,0:T(8,128)(2,1)S(1)}, bf16[16,6144]{1,0:T(8,128)(2,1)S(1)}, u32[]{:S(2)}, u32[]{:S(2)}) collective-permute-start(bf16[16,6144]{1,0:T(8,128)(2,1)S(1)} %get-tuple-element.12.refs_4_), channel_id=1, source_target_pairs={{0,1},{1,2},{2,3},{3,0},{4,5},{5,6},{6,7},{7,4},{8,9},{9,10},{10,1... | collective-permute-start | bytes 589832 | tf_op jit(solution)/shard_map/ppermute | solution.py:259
  123.8 7.6 %collective-permute-start.2 = (bf16[16,6144]{1,0:T(8,128)(2,1)S(1)}, bf16[16,6144]{1,0:T(8,128)(2,1)S(1)}, u32[]{:S(2)}, u32[]{:S(2)}) collective-permute-start(bf16[16,6144]{1,0:T(8,128)(2,1)S(1)} %collective-permute-done.refs_1_), channel_id=1, source_target_pairs={{0,1},{1,2},{2,3},{3,0},{4,5},{5,6},{6,7},{7,4},{8,9},{9,10},{10,1... | collective-permute-start | bytes 589832 | tf_op jit(solution)/shard_map/ppermute | solution.py:261
  127.7 8.8 %collective-permute-start.5 = (bf16[16,6144]{1,0:T(8,128)(2,1)S(1)}, bf16[16,6144]{1,0:T(8,128)(2,1)S(1)}, u32[]{:S(2)}, u32[]{:S(2)}) collective-permute-start(bf16[16,6144]{1,0:T(8,128)(2,1)S(1)} %collective-permute-done.4.refs_6_), channel_id=1, source_target_pairs={{0,3},{1,0},{2,1},{3,2},{4,7},{5,4},{6,5},{7,6},{8,11},{9,8},{10,9... | collective-permute-start | bytes 589832 | tf_op jit(solution)/shard_map/ppermute | solution.py:261

commit v5 on v3

--- a/solution.py
+++ b/solution.py
@@ -27,10 +27,21 @@
     return (np.asarray(source)[:, None] == np.arange(count)[None, :]).astype(jnp.bfloat16)
 
 
-def regroup(order_ref, w_ref, out_ref):
+def regroup(w_ref, out_ref, piece_ref, done_ref):
+    copies = [
+        pltpu.make_async_copy(w_ref.at[:, x], piece_ref.at[x], done_ref.at[x]) for x in range(N_X)
+    ]
+    for copy in copies:
+        copy.start()
+    size = N_F * TALL
+    row = lax.broadcasted_iota(jnp.int32, (size, size), 0)
+    col = lax.broadcasted_iota(jnp.int32, (size, size), 1)
+    source = row // C % N_F * TALL + row // (N_F * C) * C + row % C
+    order = jnp.where(col == source, 1.0, 0.0).astype(jnp.bfloat16)
     for x in range(N_X):
-        flat = w_ref[:, x].reshape(N_F * TALL, WIDE)
-        moved = jnp.dot(order_ref[...], flat, preferred_element_type=jnp.float32)
+        copies[x].wait()
+        flat = piece_ref[x].reshape(size, WIDE)
+        moved = jnp.dot(order, flat, preferred_element_type=jnp.float32)
         out_ref[:, x] = moved.astype(jnp.bfloat16).reshape(N_Y, N_F * C, WIDE)
 
 
@@ -105,16 +116,17 @@
 
 
 def regrouped(w):
-    spot = np.arange(N_F * TALL)
-    order = selection(spot // C % N_F * TALL + spot // (N_F * C) * C + spot % C, N_F * TALL)
     return pl.pallas_call(
         regroup,
-        in_specs=[VMEM, VMEM],
+        in_specs=[pl.BlockSpec(memory_space=pltpu.HBM)],
         out_specs=VMEM,
         out_shape=shape_of(N_Y, N_X, N_F * C, WIDE),
+        scratch_shapes=[
+            pltpu.VMEM((N_X, N_F, TALL, WIDE), jnp.bfloat16),
+            pltpu.SemaphoreType.DMA((N_X,)),
+        ],
         name="regroup",
-        compiler_params=pltpu.CompilerParams(vmem_limit_bytes=8 * 2**20),
-    )(order, w.reshape(N_F, N_X, TALL, WIDE))
+    )(w.reshape(N_F, N_X, TALL, WIDE))
 
 
 def picked(owner_k, got, centered):

time: 139 us -> 138 us (level)
  local copies, waits for them, and re-layouts: 2.15 us -> 0.02 us
  Pallas kernels: 4.82 us -> 6.38 us
    unnamed x12 -> x8, local copies, waits for them, and re-layouts: 2.15 us -> 0.02 us
    pallas_call x1, Pallas kernels: 1.41 us -> 2.97 us  [regrouped(): pl.pallas_call(regroup, in_specs=[pl.BlockSpec(memory_space=pltpu.HBM)],...]
where the time goes in v5:
time: 138 us; the launch traced here: 137 us
  blocking collectives  92 us (67%)
  waiting for transfers between devices  21.4 us (16%)
  starting transfers between devices  16.7 us (12%)
  Pallas kernels  6.38 us (5%)
    all_to_all x1, blocking collectives, body(): lax.all_to_all(send.reshape(N_ZH * N_F, 8, WIDE), ('zh', 'zl', 'co'), 0,...  41.6 us
    all_to_all x1, blocking collectives, body(): full = lax.all_to_all(lifted(by_y.reshape(64, LINE)), 'x', 0, 0, tiled=True)  29.5 us
    all_to_all x1, waiting for transfers between devices, body(): lax.all_to_all(regrouped(w).reshape(N_K, N_F * C, WIDE), ('y', 'x'), 0, 0...  21.4 us
    all_to_all x1, blocking collectives, body(): by_y = lax.all_to_all(lines, 'y', 0, 0, tiled=True)  20.9 us
    all_to_all x1, starting transfers between devices, body(): lax.all_to_all(regrouped(w).reshape(N_K, N_F * C, WIDE), ('y', 'x'), 0, 0...  16.7 us
    pallas_call x1, Pallas kernels, regrouped(): pl.pallas_call(regroup, in_specs=[pl.BlockSpec(memory_space=pltpu.HBM)],...  2.97 us
  transfers between devices with their start and end apart: 1, of which 1 were waited for; matrix products, arithmetic and copies ran while one was open for 0% of the time, Pallas kernels for 0%

profile of v5, /device:TPU:6, one launch (start us, length us, event | category | flops | bytes accessed | tf_op | source)
XLA Modules:
  0.0 137.4 jit_solution(3961885005462780680)
XLA Ops:
  0.6 0.0 copy-start.3
  0.6 0.0 copy-start.2
  0.6 3.0 %regroup.1 = bf16[8,4,32,512]{3,2,1,0:T(8,128)(2,1)} custom-call(bf16[16,4,16,512]{3,2,1,0:T(8,128)(2,1)} %bitcast.11), custom_call_target="tpu_custom_call" | custom-call | tf_op jit(solution)/shard_map/regroup/pallas_call | solution.py:119
  3.6 0.0 copy-start
  3.6 16.7 %all-to-all-start = ((bf16[32,32,512]{2,1,0:T(8,128)(2,1)}), bf16[32,32,512]{2,1,0:T(8,128)(2,1)S(1)}, u32[]{:S(2)}, u32[]{:S(2)}) async-start(bf16[32,32,512]{2,1,0:T(8,128)(2,1)} %bitcast.10), calls=%async_computation | async-start | bytes 2097152 | tf_op jit(solution)/shard_map/all_to_all | solution.py:187
  20.4 0.0 copy-done.3
  20.4 0.0 copy-done.2
  20.4 0.1 add_convert_fusion.centered_ref
  20.5 0.0 copy-start.1
  20.5 21.4 %all-to-all-done.got_ref = bf16[32,32,512]{2,1,0:T(8,128)(2,1)S(1)} async-done(((bf16[32,32,512]{2,1,0:T(8,128)(2,1)}), bf16[32,32,512]{2,1,0:T(8,128)(2,1)S(1)}, u32[]{:S(2)}, u32[]{:S(2)}) %all-to-all-start) | async-done | bytes 1048608 | tf_op jit(solution)/shard_map/all_to_all | solution.py:187
  41.9 0.0 copy-done
  41.9 0.9 pick.1
  42.8 41.6 %all_to_all.20 = bf16[32,8,512]{2,1,0:T(8,128)(2,1)S(1)} all-to-all(bf16[32,8,512]{2,1,0:T(8,128)(2,1)S(1)} %bitcast.8), channel_id=1, replica_groups=mesh['zl'=8,'co'=2,'y'=8,'zh'=2,'x'=4] {'zh','zl','co'}, dimensions={0} | all-to-all | bytes 524288 | tf_op jit(solution)/shard_map/all_to_all | solution.py:194
  84.5 0.7 settle.1
  85.2 20.9 %all_to_all.21 = bf16[8,8,4352]{2,1,0:T(8,128)(2,1)S(1)} all-to-all(bf16[8,8,4352]{2,1,0:T(8,128)(2,1)S(1)} %settle.1), channel_id=1, replica_groups=mesh['zl'=8,'co'=2,'y'=8,'zh'=2,'x'=4] {'y'}, dimensions={0} | all-to-all | bytes 1114112 | tf_op jit(solution)/shard_map/all_to_all | solution.py:198
  106.1 0.0 copy-done.1
  106.1 0.3 lift.1
  106.4 29.5 %all_to_all.22.full_ref = bf16[4,2,16,8704]{3,2,1,0:T(8,128)(2,1)S(1)} all-to-all(bf16[4,2,16,8704]{3,2,1,0:T(8,128)(2,1)S(1)} %lift.1), channel_id=1, replica_groups=mesh['zl'=8,'co'=2,'y'=8,'zh'=2,'x'=4] {'x'}, dimensions={0} | all-to-all | bytes 4456448 | tf_op jit(solution)/shard_map/all_to_all | solution.py:199
  135.9 1.5 %finish.1 = (bf16[2,64,8192]{2,1,0:T(8,128)(2,1)}, bf16[2,64,512]{2,1,0:T(8,128)(2,1)}) custom-call(bf16[4,2,16,8704]{3,2,1,0:T(8,128)(2,1)S(1)} %all_to_all.22.full_ref), custom_call_target="tpu_custom_call" | custom-call | tf_op jit(solution)/shard_map/finish/pallas_call | solution.py:170
  (1 shorter events, 0.0 us)
Async XLA Ops:
  0.6 19.7 %copy-start.3 = (s32[2]{0:T(128)S(1)}, s32[2]{0:T(128)}, u32[]{:S(2)}) copy-start(s32[2]{0:T(128)} %param.7) | copy-start | bytes 28
  0.6 19.8 %copy-start.2 = (s32[512,512]{1,0:T(8,128)S(1)}, s32[512,512]{1,0:T(8,128)}, u32[]{:S(2)}) copy-start(s32[512,512]{1,0:T(8,128)} %param.6) | copy-start | bytes 3145732
  3.6 38.3 %copy-start = (bf16[128,128]{1,0:T(8,128)(2,1)S(1)}, bf16[128,128]{1,0:T(8,128)(2,1)}, u32[]{:S(2)}) copy-start(bf16[128,128]{1,0:T(8,128)(2,1)} %constant.55.clone.order_ref) | copy-start | bytes 98308
  3.6 38.3 %all-to-all-start = ((bf16[32,32,512]{2,1,0:T(8,128)(2,1)}), bf16[32,32,512]{2,1,0:T(8,128)(2,1)S(1)}, u32[]{:S(2)}, u32[]{:S(2)}) async-start(bf16[32,32,512]{2,1,0:T(8,128)(2,1)} %bitcast.10), calls=%async_computation | async-start | bytes 2097152 | tf_op jit(solution)/shard_map/all_to_all | solution.py:187
  20.5 85.5 %copy-start.1 = (bf16[64,64]{1,0:T(8,128)(2,1)S(1)}, bf16[64,64]{1,0:T(8,128)(2,1)}, u32[]{:S(2)}) copy-start(bf16[64,64]{1,0:T(8,128)(2,1)} %constant.56.clone.order_ref) | copy-start | bytes 24580

commit v6 on v5

--- a/solution.py
+++ b/solution.py
@@ -27,20 +27,14 @@
     return (np.asarray(source)[:, None] == np.arange(count)[None, :]).astype(jnp.bfloat16)
 
 
-def regroup(w_ref, out_ref, piece_ref, done_ref):
-    copies = [
-        pltpu.make_async_copy(w_ref.at[:, x], piece_ref.at[x], done_ref.at[x]) for x in range(N_X)
-    ]
-    for copy in copies:
-        copy.start()
+def regroup(w_ref, out_ref):
     size = N_F * TALL
     row = lax.broadcasted_iota(jnp.int32, (size, size), 0)
     col = lax.broadcasted_iota(jnp.int32, (size, size), 1)
     source = row // C % N_F * TALL + row // (N_F * C) * C + row % C
     order = jnp.where(col == source, 1.0, 0.0).astype(jnp.bfloat16)
     for x in range(N_X):
-        copies[x].wait()
-        flat = piece_ref[x].reshape(size, WIDE)
+        flat = w_ref[:, x].reshape(size, WIDE)
         moved = jnp.dot(order, flat, preferred_element_type=jnp.float32)
         out_ref[:, x] = moved.astype(jnp.bfloat16).reshape(N_Y, N_F * C, WIDE)
 
@@ -118,14 +112,11 @@
 def regrouped(w):
     return pl.pallas_call(
         regroup,
-        in_specs=[pl.BlockSpec(memory_space=pltpu.HBM)],
+        in_specs=[VMEM],
         out_specs=VMEM,
         out_shape=shape_of(N_Y, N_X, N_F * C, WIDE),
-        scratch_shapes=[
-            pltpu.VMEM((N_X, N_F, TALL, WIDE), jnp.bfloat16),
-            pltpu.SemaphoreType.DMA((N_X,)),
-        ],
         name="regroup",
+        compiler_params=pltpu.CompilerParams(vmem_limit_bytes=8 * 2**20),
     )(w.reshape(N_F, N_X, TALL, WIDE))
 
 

time: 138 us -> 138 us (level)
  Pallas kernels: 6.38 us -> 4.83 us
    pallas_call x1, Pallas kernels: 2.97 us -> 1.42 us  [regrouped(): pl.pallas_call(regroup, in_specs=[VMEM], out_specs=VMEM, out_shape=shape_...]
where the time goes in v6:
time: 138 us; the launch traced here: 137 us
  blocking collectives  92 us (67%)
  waiting for transfers between devices  21.4 us (16%)
  starting transfers between devices  16.8 us (12%)
  Pallas kernels  4.83 us (4%)
    all_to_all x1, blocking collectives, body(): lax.all_to_all(send.reshape(N_ZH * N_F, 8, WIDE), ('zh', 'zl', 'co'), 0,...  41.6 us
    all_to_all x1, blocking collectives, body(): full = lax.all_to_all(lifted(by_y.reshape(64, LINE)), 'x', 0, 0, tiled=True)  29.5 us
    all_to_all x1, waiting for transfers between devices, body(): lax.all_to_all(regrouped(w).reshape(N_K, N_F * C, WIDE), ('y', 'x'), 0, 0...  21.4 us
    all_to_all x1, blocking collectives, body(): by_y = lax.all_to_all(lines, 'y', 0, 0, tiled=True)  20.9 us
    all_to_all x1, starting transfers between devices, body(): lax.all_to_all(regrouped(w).reshape(N_K, N_F * C, WIDE), ('y', 'x'), 0, 0...  16.8 us
  transfers between devices with their start and end apart: 1, of which 1 were waited for; matrix products, arithmetic and copies ran while one was open for 0% of the time, Pallas kernels for 0%

profile of v6, /device:TPU:6, one launch (start us, length us, event | category | flops | bytes accessed | tf_op | source)
XLA Modules:
  0.0 137.1 jit_solution(10300198626001413863)
XLA Ops:
  0.6 0.0 copy-start.4
  0.6 0.0 copy-start
  0.6 1.2 copy-done
  1.9 0.0 copy-start.3
  1.9 1.4 %regroup.1 = bf16[8,4,32,512]{3,2,1,0:T(8,128)(2,1)} custom-call(bf16[16,4,16,512]{3,2,1,0:T(8,128)(2,1)S(1)} %bitcast.8), custom_call_target="tpu_custom_call" | custom-call | tf_op jit(solution)/shard_map/regroup/pallas_call | solution.py:113
  3.3 0.0 copy-start.1
  3.3 16.8 %all-to-all-start = ((bf16[32,32,512]{2,1,0:T(8,128)(2,1)}), bf16[32,32,512]{2,1,0:T(8,128)(2,1)S(1)}, u32[]{:S(2)}, u32[]{:S(2)}) async-start(bf16[32,32,512]{2,1,0:T(8,128)(2,1)} %bitcast.1), calls=%async_computation | async-start | bytes 2097152 | tf_op jit(solution)/shard_map/all_to_all | solution.py:178
  20.1 0.0 copy-done.4
  20.2 0.0 copy-done.3
  20.2 0.1 add_convert_fusion.centered_ref
  20.3 0.0 copy-start.2
  20.3 21.4 %all-to-all-done.got_ref = bf16[32,32,512]{2,1,0:T(8,128)(2,1)S(1)} async-done(((bf16[32,32,512]{2,1,0:T(8,128)(2,1)}), bf16[32,32,512]{2,1,0:T(8,128)(2,1)S(1)}, u32[]{:S(2)}, u32[]{:S(2)}) %all-to-all-start) | async-done | bytes 1048608 | tf_op jit(solution)/shard_map/all_to_all | solution.py:178
  41.7 0.0 copy-done.1
  41.7 0.9 pick.1
  42.6 41.6 %all_to_all.20 = bf16[32,8,512]{2,1,0:T(8,128)(2,1)S(1)} all-to-all(bf16[32,8,512]{2,1,0:T(8,128)(2,1)S(1)} %bitcast.9), channel_id=1, replica_groups=mesh['zl'=8,'co'=2,'y'=8,'zh'=2,'x'=4] {'zh','zl','co'}, dimensions={0} | all-to-all | bytes 524288 | tf_op jit(solution)/shard_map/all_to_all | solution.py:185
  84.2 0.7 settle.1
  85.0 20.9 %all_to_all.21 = bf16[8,8,4352]{2,1,0:T(8,128)(2,1)S(1)} all-to-all(bf16[8,8,4352]{2,1,0:T(8,128)(2,1)S(1)} %settle.1), channel_id=1, replica_groups=mesh['zl'=8,'co'=2,'y'=8,'zh'=2,'x'=4] {'y'}, dimensions={0} | all-to-all | bytes 1114112 | tf_op jit(solution)/shard_map/all_to_all | solution.py:189
  105.8 0.0 copy-done.2
  105.8 0.3 lift.1
  106.1 29.5 %all_to_all.22.full_ref = bf16[4,2,16,8704]{3,2,1,0:T(8,128)(2,1)S(1)} all-to-all(bf16[4,2,16,8704]{3,2,1,0:T(8,128)(2,1)S(1)} %lift.1), channel_id=1, replica_groups=mesh['zl'=8,'co'=2,'y'=8,'zh'=2,'x'=4] {'x'}, dimensions={0} | all-to-all | bytes 4456448 | tf_op jit(solution)/shard_map/all_to_all | solution.py:190
  135.7 1.5 %finish.1 = (bf16[2,64,8192]{2,1,0:T(8,128)(2,1)}, bf16[2,64,512]{2,1,0:T(8,128)(2,1)}) custom-call(bf16[4,2,16,8704]{3,2,1,0:T(8,128)(2,1)S(1)} %all_to_all.22.full_ref), custom_call_target="tpu_custom_call" | custom-call | tf_op jit(solution)/shard_map/finish/pallas_call | solution.py:161
  (1 shorter events, 0.0 us)
Async XLA Ops:
  0.6 19.5 %copy-start.4 = (s32[2]{0:T(128)S(1)}, s32[2]{0:T(128)}, u32[]{:S(2)}) copy-start(s32[2]{0:T(128)} %param.7) | copy-start | bytes 28
  0.6 1.2 copy-start
  1.9 18.3 %copy-start.3 = (s32[512,512]{1,0:T(8,128)S(1)}, s32[512,512]{1,0:T(8,128)}, u32[]{:S(2)}) copy-start(s32[512,512]{1,0:T(8,128)} %param.6) | copy-start | bytes 3145732
  3.3 38.4 %copy-start.1 = (bf16[128,128]{1,0:T(8,128)(2,1)S(1)}, bf16[128,128]{1,0:T(8,128)(2,1)}, u32[]{:S(2)}) copy-start(bf16[128,128]{1,0:T(8,128)(2,1)} %constant.55.clone.order_ref) | copy-start | bytes 98308
  3.3 38.4 %all-to-all-start = ((bf16[32,32,512]{2,1,0:T(8,128)(2,1)}), bf16[32,32,512]{2,1,0:T(8,128)(2,1)S(1)}, u32[]{:S(2)}, u32[]{:S(2)}) async-start(bf16[32,32,512]{2,1,0:T(8,128)(2,1)} %bitcast.1), calls=%async_computation | async-start | bytes 2097152 | tf_op jit(solution)/shard_map/all_to_all | solution.py:178
  20.3 85.5 %copy-start.2 = (bf16[64,64]{1,0:T(8,128)(2,1)S(1)}, bf16[64,64]{1,0:T(8,128)(2,1)}, u32[]{:S(2)}) copy-start(bf16[64,64]{1,0:T(8,128)(2,1)} %constant.56.clone.order_ref) | copy-start | bytes 24580
